TPU v7x, 16 devices: a 4x2x1 block of a 4x4x8 slice. The times are simulated.
16 devices in a mesh: dp: 2 (over y, z), tp: 8 (over x, core).
Axes of the slice: x: 4, y: 2, z: 1, core: 2. Of those that a mesh axis runs over, the one named last changes fastest.
The devices are a block of a 4x4x8 slice.
Arguments:
- x_in: bfloat16 [2, 4096, 2048], P('dp', 'tp'), parts along dimension 0
- cond_vec: bfloat16 [2, 2048], P('dp'), parts along dimension 0
- rope_cos: float32 [4096, 128], P('tp')
- rope_sin: float32 [4096, 128], P('tp')
- w_mod: bfloat16 [2, 2048, 6144], replicated
- b_mod: bfloat16 [2, 6144], replicated
- w_in: bfloat16 [2, 2048, 8, 1792], P(None, None, 'tp')
- b_in: bfloat16 [2, 8, 1792], P(None, 'tp')
- q_scale: bfloat16 [2, 256], replicated
- k_scale: bfloat16 [2, 256], replicated
- w_out: bfloat16 [2, 8, 1280, 2048], P(None, 'tp')
- b_out: bfloat16 [2, 2048], replicated
- d_out: bfloat16 [2, 4096, 2048], P('dp', 'tp'), parts along dimension 0
Outputs:
- output 1: bfloat16 [2, 4096, 2048], P('dp', 'tp'), parts along dimension 0
- output 2: bfloat16 [2, 4096, 2048], P('dp', 'tp'), parts along dimension 0
- output 3: float32 [4, 2048, 6144], P('dp'), parts along dimension 0
- output 4: float32 [4, 6144], P('dp'), parts along dimension 0
- output 5: bfloat16 [4, 2048, 8, 1792], P('dp', None, 'tp'), parts along dimension 0
- output 6: float32 [4, 8, 1792], P('dp', 'tp'), parts along dimension 0
- output 7: float32 [4, 256], P('dp'), parts along dimension 0
- output 8: float32 [4, 256], P('dp'), parts along dimension 0
- output 9: bfloat16 [4, 8, 1280, 2048], P('dp', 'tp'), parts along dimension 0
- output 10: float32 [4, 2048], P('dp'), parts along dimension 0
There are 2 independent parts. A program takes and returns all parts, laid end to end along the dimension named above; an argument that names none is the same for every part.
All inputs are finite; a program needn't handle non-finite values.
Results may differ from a plain program's by a relative error of at most 0.02.
Values are sent between devices in bfloat16 or wider.
A program may use at most 768 MiB of HBM per device.

v0:
```python
import functools
import jax
import jax.numpy as jnp
from jax import lax
from jax.sharding import PartitionSpec as P

NORM_EPS = 1e-6


def rms_norm(tensor):
    return tensor * lax.rsqrt(jnp.mean(tensor * tensor, axis=-1, keepdims=True) + NORM_EPS)


def apply_rope(tensor, rope_cos, rope_sin):
    pair_view = tensor.reshape(tensor.shape[:-1] + (tensor.shape[-1] // 2, 2))
    even_part = pair_view[..., 0]
    odd_part = pair_view[..., 1]
    cos_wide = rope_cos[None, :, None, :]
    sin_wide = rope_sin[None, :, None, :]
    rotated = jnp.stack([even_part * cos_wide - odd_part * sin_wide, even_part * sin_wide + odd_part * cos_wide], axis=-1)
    return rotated.reshape(tensor.shape)


def layer_modulate(x_f32, mod_shift, mod_scale):
    row_mean = jnp.mean(x_f32, axis=-1, keepdims=True)
    centered = x_f32 - row_mean
    row_var = jnp.mean(centered * centered, axis=-1, keepdims=True)
    normed = centered * lax.rsqrt(row_var + NORM_EPS)
    return (normed * (1.0 + mod_scale[:, None, :]) + mod_shift[:, None, :]).astype(jnp.bfloat16)


def mix_heads(projected, q_scale, k_scale, rope_cos, rope_sin):
    head_dim = q_scale.shape[-1]
    q_rot = apply_rope(rms_norm(projected[..., :head_dim]) * q_scale, rope_cos, rope_sin).astype(jnp.bfloat16)
    k_rot = apply_rope(rms_norm(projected[..., head_dim:2 * head_dim]) * k_scale, rope_cos, rope_sin).astype(jnp.bfloat16)
    v_part = projected[..., 2 * head_dim:3 * head_dim].astype(jnp.bfloat16)
    scores = jnp.einsum("bqhe,bkhe->bhqk", q_rot, k_rot, preferred_element_type=jnp.float32) * (head_dim ** -0.5)
    attn_probs = jax.nn.softmax(scores, axis=-1).astype(jnp.bfloat16)
    attn_out = jnp.einsum("bhqk,bkhe->bqhe", attn_probs, v_part, preferred_element_type=jnp.float32).astype(jnp.bfloat16)
    mlp_act = jax.nn.gelu(projected[..., 3 * head_dim:], approximate=True).astype(jnp.bfloat16)
    return jnp.concatenate([attn_out, mlp_act], axis=-1)


def solution(mesh):
    act_spec = P("dp", "tp", None)
    in_specs = (act_spec, P("dp", None), P("tp", None), P("tp", None), P(None, None, None), P(None, None), P(None, None, "tp", None), P(None, "tp", None), P(None, None), P(None, None), P(None, "tp", None, None), P(None, None), act_spec)
    out_specs = (act_spec, act_spec, P("dp", None, None), P("dp", None), P("dp", None, "tp", None), P("dp", "tp", None), P("dp", None), P("dp", None), P("dp", "tp", None, None), P("dp", None))

    def device_fn(x_in, cond_vec, rope_cos, rope_sin, w_mod, b_mod, w_in, b_in, q_scale, k_scale, w_out, b_out, d_out):
        num_blocks = w_in.shape[0]
        cos_full = lax.all_gather(rope_cos, "tp", axis=0, tiled=True)
        sin_full = lax.all_gather(rope_sin, "tp", axis=0, tiled=True)
        core_fn = functools.partial(mix_heads, rope_cos=cos_full, rope_sin=sin_full)
        silu_vec = jax.nn.silu(cond_vec.astype(jnp.float32)).astype(jnp.bfloat16)
        saved_acts = []
        x_cur = x_in
        for block_idx in range(num_blocks):
            mod_vec = jnp.dot(silu_vec, w_mod[block_idx], preferred_element_type=jnp.float32) + b_mod[block_idx].astype(jnp.float32)
            mod_shift, mod_scale, mod_gate = jnp.split(mod_vec, 3, axis=-1)
            x_f32 = x_cur.astype(jnp.float32)
            normed = layer_modulate(x_f32, mod_shift, mod_scale)
            normed_full = lax.all_gather(normed, "tp", axis=1, tiled=True)
            projected = jnp.einsum("bsd,dhc->bshc", normed_full, w_in[block_idx], preferred_element_type=jnp.float32) + b_in[block_idx].astype(jnp.float32)
            joined = core_fn(projected, q_scale[block_idx].astype(jnp.float32), k_scale[block_idx].astype(jnp.float32))
            part_out = jnp.einsum("bshc,hcd->bsd", joined, w_out[block_idx], preferred_element_type=jnp.float32)
            mixed_out = lax.psum_scatter(part_out.astype(jnp.bfloat16), "tp", scatter_dimension=1, tiled=True)
            branch = mixed_out.astype(jnp.float32) + b_out[block_idx].astype(jnp.float32)
            saved_acts.append((x_f32, mod_vec, normed_full, projected, joined, branch))
            x_cur = (x_f32 + mod_gate[:, None, :] * branch).astype(jnp.bfloat16)
        x_out = x_cur

        silu_f32 = silu_vec.astype(jnp.float32)
        grad_cur = d_out
        block_grads = {}
        for block_idx in reversed(range(num_blocks)):
            x_f32, mod_vec, normed_full, projected, joined, branch = saved_acts[block_idx]
            mod_shift, mod_scale, mod_gate = jnp.split(mod_vec, 3, axis=-1)
            qs_f32 = q_scale[block_idx].astype(jnp.float32)
            ks_f32 = k_scale[block_idx].astype(jnp.float32)
            grad_f32 = grad_cur.astype(jnp.float32)
            d_gate = jnp.sum(grad_f32 * branch, axis=1)
            gated_grad = grad_f32 * mod_gate[:, None, :]
            d_bout = lax.psum(jnp.sum(gated_grad, axis=(0, 1)), "tp")
            d_branch = lax.all_gather(gated_grad.astype(jnp.bfloat16), "tp", axis=1, tiled=True)
            g_wout = jnp.einsum("bshc,bsd->hcd", joined, d_branch, preferred_element_type=jnp.float32).astype(jnp.bfloat16)
            d_joined = jnp.einsum("bsd,hcd->bshc", d_branch, w_out[block_idx], preferred_element_type=jnp.float32).astype(jnp.bfloat16)
            unused_out, core_pull = jax.vjp(core_fn, projected, qs_f32, ks_f32)
            d_proj, d_qs, d_ks = core_pull(d_joined)
            g_bin = jnp.sum(d_proj, axis=(0, 1))
            d_proj16 = d_proj.astype(jnp.bfloat16)
            g_win = jnp.einsum("bsd,bshc->dhc", normed_full, d_proj16, preferred_element_type=jnp.float32).astype(jnp.bfloat16)
            d_norm_part = jnp.einsum("bshc,dhc->bsd", d_proj16, w_in[block_idx], preferred_element_type=jnp.float32)
            d_normed = lax.psum_scatter(d_norm_part.astype(jnp.bfloat16), "tp", scatter_dimension=1, tiled=True)
            unused_norm, norm_pull = jax.vjp(layer_modulate, x_f32, mod_shift, mod_scale)
            d_xnorm, d_shift, d_scale = norm_pull(d_normed)
            d_mod = lax.psum(jnp.concatenate([d_shift, d_scale, d_gate], axis=-1), "tp")
            g_wmod = jnp.einsum("bd,bm->dm", silu_f32, d_mod, preferred_element_type=jnp.float32)
            block_grads[block_idx] = (g_wmod, jnp.sum(d_mod, axis=0), g_win, g_bin, lax.psum(d_qs, "tp"), lax.psum(d_ks, "tp"), g_wout, d_bout)
            grad_cur = (grad_f32 + d_xnorm).astype(jnp.bfloat16)
        stacked = tuple(jnp.stack([block_grads[block_idx][entry_idx] for block_idx in range(num_blocks)]) for entry_idx in range(8))
        return (x_out, grad_cur) + stacked

    return jax.shard_map(device_fn, mesh=mesh, in_specs=in_specs, out_specs=out_specs, check_vma=False)
```

profile of v0, /device:TPU:113, one launch (start us, length us, event | category | flops | bytes accessed | tf_op | source)
XLA Modules:
  0.0 2055.1 jit_solution(17430563064208081555)
XLA Ops:
  29.7 80.6 %all-gather.7.cloned.1.call-done = bf16[1,4096,2048]{2,1,0:T(8,128)(2,1)} async-done(((bf16[1,512,2048]{2,1,0:T(8,128)(2,1)}), bf16[1,4096,2048]{2,1,0:T(8,128)(2,1)}) %all-gather.7.cloned.1.call-update) | async-done | bytes 16777232 | tf_op jit(solution)/shard_map/all_gather | solution.py:62
  110.3 38.7 %add_bitcast_fusion.1 = f32[1,4096,1,1792]{1,3,2,0:T(8,128)} fusion(bf16[1,4096,2048]{2,1,0:T(8,128)(2,1)} %all-gather.7.cloned.1.call-done, f32[1792]{0:T(1024)S(1)} %get-tuple-element.39, bf16[2,2048,1,1792]{3,1,2,0:T(8,128)(2,1)} %param.19), kind=kOutput, calls=%fused_computation.32 | convolution fusion | flops 30072111104 | bytes 53484544 | tf_op jit(solution)/shard_map/bsd,dhc->bshc/dot_general | solution.py:63
  275.3 33.3 %divide_convert_fusion.1 = bf16[4096,4096]{0,1:T(8,128)(2,1)} fusion(f32[4096]{0:T(1024)S(1)} %fusion.12, f32[4096]{0:T(1024)S(1)} %get-tuple-element.123, f32[4096,4096,1]{0,1,2:T(8,128)} %get-tuple-element.124), kind=kLoop, calls=%fused_computation.19 | loop fusion | flops 67108864 | bytes 100696064 | tf_op jit(solution)/shard_map/convert_element_type | solution.py:38
  326.3 29.1 %convert_bitcast_fusion.3 = bf16[1,4096,2048]{2,1,0:T(8,128)(2,1)} fusion(bf16[1,4096,1,1024]{1,3,2,0:T(8,128)(2,1)} %multiply_convert_fusion.1, bf16[1,4096,1,256]{1,3,2,0:T(8,128)(2,1)S(1)} %fusion.136, bf16[2,1,1280,2048]{3,2,1,0:T(8,128)(2,1)} %param.23), kind=kOutput, calls=%fused_computation.83 | convolution fusion | flops 21504196608 | bytes 32505856 | tf_op jit(solution)/shard_map/bshc,hcd->bsd/dot_general | solution.py:65
  369.3 73.7 %reduce-scatter.5.cloned.1.call-done = bf16[1,512,2048]{2,1,0:T(8,128)(2,1)} async-done(((bf16[1,4096,2048]{2,1,0:T(8,128)(2,1)}), bf16[1,512,2048]{2,1,0:T(8,128)(2,1)}) %reduce-scatter.5.cloned.1.call-update) | async-done | bytes 2097168 | tf_op jit(solution)/shard_map/reduce_scatter | solution.py:66
  449.3 77.3 %all-gather.15.cloned.1.call-done = bf16[1,4096,2048]{2,1,0:T(8,128)(2,1)} async-done(((bf16[1,512,2048]{2,1,0:T(8,128)(2,1)}), bf16[1,4096,2048]{2,1,0:T(8,128)(2,1)}) %all-gather.15.cloned.1.call-update) | async-done | bytes 16777232 | tf_op jit(solution)/shard_map/all_gather | solution.py:84
  554.6 55.7 %all-gather.13.cloned.1.call-done = bf16[1,4096,2048]{2,1,0:T(8,128)(2,1)} async-done(((bf16[1,512,2048]{2,1,0:T(8,128)(2,1)}), bf16[1,4096,2048]{2,1,0:T(8,128)(2,1)}) %all-gather.13.cloned.1.call-update) | async-done | bytes 16777232 | tf_op jit(solution)/shard_map/all_gather | solution.py:62
  610.3 38.6 %add_bitcast_fusion = f32[1,4096,1,1792]{1,3,2,0:T(8,128)} fusion(bf16[1,4096,2048]{2,1,0:T(8,128)(2,1)} %all-gather.13.cloned.1.call-done, f32[1792]{0:T(1024)S(1)} %copy-done.103, bf16[2,2048,1,1792]{3,1,2,0:T(8,128)(2,1)} %param.19), kind=kOutput, calls=%fused_computation.31 | convolution fusion | flops 30072111104 | bytes 53484544 | tf_op jit(solution)/shard_map/bsd,dhc->bshc/dot_general | solution.py:63
  802.0 48.7 %fusion.4 = (f32[4096]{0:T(1024)S(1)}, bf16[4096,4096]{0,1:T(8,128)(2,1)}, bf16[4096,4096]{0,1:T(8,128)(2,1)}) fusion(f32[4096]{0:T(1024)S(1)} %multiply_divide_fusion.1, f32[4096]{0:T(1024)S(1)} %get-tuple-element.125, f32[4096,4096,1]{0,1,2:T(8,128)} %get-tuple-element.126, f32[4096]{0:T(1024)S(1)} %fusion.13, f32[1,4096,1,1792]{1,3,2,0:T(8,128)} %add_bitcast_fusion, ...), kind=kOutput, calls=%fused_computation.9 | convolution fusion | flops 8740925440 | bytes 138477568 | tf_op jit(solution)/shard_map/transpose(jvp(bhqk,bkhe->bqhe))/dot_general | solution.py:39
  850.7 43.8 %fusion.2 = bf16[4096,4096]{0,1:T(8,128)(2,1)} fusion(bf16[4096,4096]{0,1:T(8,128)(2,1)} %get-tuple-element.127, f32[4096]{0:T(1024)S(1)} %neg.41, f32[4096]{0:T(1024)S(1)} %fusion.13, f32[4096]{0:T(1024)S(1)} %get-tuple-element.125, f32[4096,4096,1]{0,1,2:T(8,128)} %get-tuple-element.126), kind=kLoop, calls=%fused_computation.7 | loop fusion | flops 134217728 | bytes 134266880 | tf_op jit(solution)/shard_map/transpose(jvp())/mul | solution.py:37
  1066.7 41.0 %convert_bitcast_fusion.1 = bf16[1,4096,2048]{2,1,0:T(8,128)(2,1)} fusion(bf16[2,2048,1,1792]{3,1,2,0:T(8,128)(2,1)} %param.19, f32[1,4096,1,256]{1,3,2,0:T(8,128)} %get-tuple-element.58, f32[1,4096,1,256]{1,3,2,0:T(8,128)} %get-tuple-element.57, bf16[1,4096,1,256]{1,3,2,0:T(8,128)(2,1)S(1)} %fusion.134, f32[1,4096,1,1024]{1,3,2,0:T(8,128)} %get-tuple-element.55), kind=kOutput, calls=%fused_computation.80 | convolution fusion | flops 30109859840 | bytes 51380224 | tf_op jit(solution)/shard_map/bshc,dhc->bsd/dot_general | solution.py:92
  1125.8 28.6 %convert_bitcast_fusion.2 = bf16[1,4096,2048]{2,1,0:T(8,128)(2,1)} fusion(bf16[1,4096,1,1024]{1,3,2,0:T(8,128)(2,1)} %get-tuple-element.56, bf16[1,4096,1,256]{1,3,2,0:T(8,128)(2,1)S(1)} %fusion.137, bf16[2,1,1280,2048]{3,2,1,0:T(8,128)(2,1)} %param.23), kind=kOutput, calls=%fused_computation.81 | convolution fusion | flops 21504196608 | bytes 32505856 | tf_op jit(solution)/shard_map/bshc,hcd->bsd/dot_general | solution.py:65
  1154.6 40.7 %reduce-scatter.9.cloned.1.call-done = bf16[1,512,2048]{2,1,0:T(8,128)(2,1)} async-done(((bf16[1,4096,2048]{2,1,0:T(8,128)(2,1)}), bf16[1,512,2048]{2,1,0:T(8,128)(2,1)}) %reduce-scatter.9.cloned.1.call-update) | async-done | bytes 2097168 | tf_op jit(solution)/shard_map/reduce_scatter | solution.py:93
  1201.7 83.5 %reduce-scatter.7.cloned.1.call-done = bf16[1,512,2048]{2,1,0:T(8,128)(2,1)} async-done(((bf16[1,4096,2048]{2,1,0:T(8,128)(2,1)}), bf16[1,512,2048]{2,1,0:T(8,128)(2,1)}) %reduce-scatter.7.cloned.1.call-update) | async-done | bytes 2097168 | tf_op jit(solution)/shard_map/reduce_scatter | solution.py:66
  1317.6 60.7 %all-gather.17.cloned.1.call-done = bf16[1,4096,2048]{2,1,0:T(8,128)(2,1)} async-done(((bf16[1,512,2048]{2,1,0:T(8,128)(2,1)}), bf16[1,4096,2048]{2,1,0:T(8,128)(2,1)}) %all-gather.17.cloned.1.call-update) | async-done | bytes 16777232 | tf_op jit(solution)/shard_map/all_gather | solution.py:84
  1442.1 37.5 %fusion.9 = (f32[4096]{0:T(1024)S(1)}, bf16[4096,4096]{0,1:T(8,128)(2,1)}) fusion(f32[4096]{0:T(1024)S(1)} %multiply_divide_fusion, f32[4096]{0:T(1024)S(1)} %copy-done.51, f32[4096,4096,1]{0,1,2:T(8,128)} %get-tuple-element.124, f32[1,4096,1,1792]{1,3,2,0:T(8,128)} %add_bitcast_fusion.1, bf16[1,4096,1,1280]{1,3,2,0:T(8,128)(2,1)} %fusion.66), kind=kOutput, calls=%fused_computation.14 | convolution fusion | flops 8707371008 | bytes 104906752 | tf_op jit(solution)/shard_map/transpose(jvp(bhqk,bkhe->bqhe))/dot_general | solution.py:39
  1479.6 43.6 %fusion.7 = bf16[4096,4096]{0,1:T(8,128)(2,1)} fusion(bf16[4096,4096]{0,1:T(8,128)(2,1)} %get-tuple-element.129, f32[4096]{0:T(1024)S(1)} %neg.45, f32[4096]{0:T(1024)S(1)} %copy-done.49, f32[4096]{0:T(1024)S(1)} %copy-done.51, f32[4096,4096,1]{0,1,2:T(8,128)} %get-tuple-element.124), kind=kLoop, calls=%fused_computation.12 | loop fusion | flops 134217728 | bytes 134266880 | tf_op jit(solution)/shard_map/transpose(jvp())/mul | solution.py:37
  1665.4 41.2 %convert_bitcast_fusion = bf16[1,4096,2048]{2,1,0:T(8,128)(2,1)} fusion(bf16[2,2048,1,1792]{3,1,2,0:T(8,128)(2,1)} %param.19, f32[1,4096,1,256]{1,3,2,0:T(8,128)} %get-tuple-element.54, f32[1,4096,1,256]{1,3,2,0:T(8,128)} %get-tuple-element.53, bf16[1,4096,1,256]{1,3,2,0:T(8,128)(2,1)S(1)} %copy-done.36, f32[1,4096,1,1024]{1,3,2,0:T(8,128)} %fusion.25), kind=kOutput, calls=%fused_computation.79 | convolution fusion | flops 30109859840 | bytes 51380224 | tf_op jit(solution)/shard_map/bshc,dhc->bsd/dot_general | solution.py:92
  1747.8 46.3 %fusion.92 = bf16[1,2048,1,1792]{3,1,2,0:T(8,128)(2,1)} fusion(bf16[1,4096,2048]{2,1,0:T(8,128)(2,1)} %all-gather.13.cloned.1.call-done, f32[1,4096,1,256]{1,3,2,0:T(8,128)S(1)} %copy-done.14, f32[1,4096,1,256]{1,3,2,0:T(8,128)S(1)} %copy-done.13, bf16[1,4096,1,256]{1,3,2,0:T(8,128)(2,1)} %copy-done.34, f32[1,4096,1,1024]{1,3,2,0:T(8,128)} %get-tuple-element.55), kind=kOutput, calls=%fused_computation.109 | convolution fusion | flops 30105141248 | bytes 51380224 | tf_op jit(solution)/shard_map/bsd,bshc->dhc/dot_general | solution.py:91
  1805.6 28.5 %fusion.102 = bf16[1,1,1280,2048]{3,2,1,0:T(8,128)(2,1)} fusion(bf16[1,4096,2048]{2,1,0:T(8,128)(2,1)} %all-gather.17.cloned.1.call-done, bf16[1,4096,1,1024]{1,3,2,0:T(8,128)(2,1)} %multiply_convert_fusion.1, bf16[1,4096,1,256]{1,3,2,0:T(8,128)(2,1)S(1)} %copy-done.107), kind=kOutput, calls=%fused_computation.111 | convolution fusion | flops 21498429440 | bytes 32505856 | tf_op jit(solution)/shard_map/bshc,bsd->hcd/dot_general | solution.py:85
  1843.3 36.1 %fusion.97 = bf16[1,2048,1,1792]{3,1,2,0:T(8,128)(2,1)S(1)} fusion(bf16[1,4096,2048]{2,1,0:T(8,128)(2,1)} %all-gather.7.cloned.1.call-done, f32[1,4096,1,256]{1,3,2,0:T(8,128)} %get-tuple-element.54, f32[1,4096,1,256]{1,3,2,0:T(8,128)} %get-tuple-element.53, bf16[1,4096,1,256]{1,3,2,0:T(8,128)(2,1)S(1)} %copy-done.37, f32[1,4096,1,1024]{1,3,2,0:T(8,128)} %fusion.25), kind=kOutput, calls=%fused_computation.110 | convolution fusion | flops 30105141248 | bytes 51380224 | tf_op jit(solution)/shard_map/bsd,bshc->dhc/dot_general | solution.py:91
  1899.7 45.3 %all-reduce.19.cloned.1.call-done = (f32[1,6144]{1,0:T(1,128)}, f32[1,6144]{1,0:T(1,128)}, f32[1,256]{1,0:T(1,128)}, f32[1,256]{1,0:T(1,128)}, f32[1,256]{1,0:T(...) async-done(((f32[1,6144]{1,0:T(1,128)}, f32[1,6144]{1,0:T(1,128)}, f32[1,256]{1,0:T(1,128)}, f32[1,256]{1,0:T(1,128)}, f32[1,256]{1,0:T(1,128)}, ...) | async-done | bytes 69648 | tf_op jit(solution)/shard_map/psum | solution.py:96
  1950.2 32.9 %multiply_bitcast_fusion.1 = (f32[1,2048,6144]{2,1,0:T(8,128)}, f32[1,2048,6144]{2,1,0:T(8,128)}) fusion(f32[6144]{0:T(1024)} %bitcast.521, f32[2048]{0:T(1024)S(1)} %copy-done.81, f32[6144]{0:T(1024)} %bitcast.520), kind=kLoop, calls=%fused_computation.24 | loop fusion | flops 25165824 | bytes 100720640 | tf_op jit(solution)/shard_map/stack | solution.py:100
  1983.1 65.2 %pad_maximum_fusion = f32[2,2048,6144]{2,1,0:T(8,128)} fusion(f32[1,2048,6144]{2,1,0:T(8,128)} %get-tuple-element.116, f32[1,2048,6144]{2,1,0:T(8,128)} %get-tuple-element.115), kind=kLoop, calls=%fused_computation | loop fusion | flops 25165824 | bytes 201326592 | tf_op jit(solution)/shard_map/stack | solution.py:100
  (390 shorter events, 889.3 us)
Async XLA Ops:
  7.2 103.1 %all-gather.7.cloned.1.call-start = ((), (), s32[]{:S(2)}) async-start(), calls=%async_computation.4 | async-start | bytes 18874368 | tf_op jit(solution)/shard_map/all_gather | solution.py:62
  25.7 197.1 %all-gather.11.cloned.1.call-start = ((), (), s32[]{:S(2)}) async-start(), calls=%async_computation.6 | async-start | bytes 2359296 | tf_op jit(solution)/shard_map/all_gather | solution.py:52
  26.5 196.3 %all-gather.9.cloned.1.call-start = ((), (), s32[]{:S(2)}) async-start(), calls=%async_computation.5 | async-start | bytes 2359296 | tf_op jit(solution)/shard_map/all_gather | solution.py:51
  27.3 415.6 %reduce-scatter.5.cloned.1.call-start = ((), (), s32[]{:S(2)}) async-start(), calls=%async_computation.7 | async-start | bytes 18874368 | tf_op jit(solution)/shard_map/reduce_scatter | solution.py:66
  29.1 124.7 %copy-start.95 = (f32[1,256]{1,0:T(1,128)}, f32[1,256]{1,0:T(1,128)S(1)}, u32[]{:S(2)}) copy-start(f32[1,256]{1,0:T(1,128)S(1)} %get-tuple-element.122) | copy-start | bytes 3076
  29.7 124.1 %copy-start.97 = (f32[1,256]{1,0:T(1,128)}, f32[1,256]{1,0:T(1,128)S(1)}, u32[]{:S(2)}) copy-start(f32[1,256]{1,0:T(1,128)S(1)} %get-tuple-element.120) | copy-start | bytes 3076
  355.4 171.2 %all-gather.15.cloned.1.call-start = ((), (), s32[]{:S(2)}) async-start(), calls=%async_computation.10 | async-start | bytes 18874368 | tf_op jit(solution)/shard_map/all_gather | solution.py:84
  366.1 76.9 %copy-start.1 = (bf16[1,512,2048]{2,1,0:T(8,128)(2,1)S(1)}, bf16[1,512,2048]{2,1,0:T(8,128)(2,1)}, u32[]{:S(2)}) copy-start(bf16[1,512,2048]{2,1,0:T(8,128)(2,1)} %param.13) | copy-start | bytes 6291460
  366.1 76.9 %copy-start.64 = (f32[1,2048]{1,0:T(1,128)S(1)}, f32[1,2048]{1,0:T(1,128)}, u32[]{:S(2)}) copy-start(f32[1,2048]{1,0:T(1,128)} %get-tuple-element.112) | copy-start | bytes 24580
  366.1 80.4 %copy-start.52 = (f32[1,2048]{1,0:T(1,128)}, f32[1,2048]{1,0:T(1,128)S(1)}, u32[]{:S(2)}) copy-start(f32[1,2048]{1,0:T(1,128)S(1)} %get-tuple-element.109) | copy-start | bytes 24580
  368.6 241.7 %all-gather.13.cloned.1.call-start = ((), (), s32[]{:S(2)}) async-start(), calls=%async_computation.8 | async-start | bytes 18874368 | tf_op jit(solution)/shard_map/all_gather | solution.py:62
  369.3 77.2 %copy-start.75 = (f32[1,2048]{1,0:T(1,128)}, f32[1,2048]{1,0:T(1,128)S(1)}, u32[]{:S(2)}) copy-start(f32[1,2048]{1,0:T(1,128)S(1)} %get-tuple-element.118) | copy-start | bytes 24580
  446.5 108.2 %copy-start.93 = (f32[512]{0:T(512)}, f32[512]{0:T(512)S(1)}, u32[]{:S(2)}) copy-start(f32[512]{0:T(512)S(1)} %fusion.151) | copy-start | bytes 6148
  446.5 108.1 %copy-start.79 = (f32[512]{0:T(512)}, f32[512]{0:T(512)S(1)}, u32[]{:S(2)}) copy-start(f32[512]{0:T(512)S(1)} %fusion.227) | copy-start | bytes 6148
  449.3 161.0 %copy-start.103 = (f32[1792]{0:T(1024)S(1)}, f32[1792]{0:T(1024)}, u32[]{:S(2)}) copy-start(f32[1792]{0:T(1024)} %get-tuple-element.38) | copy-start | bytes 21508
  449.3 746.1 %reduce-scatter.9.cloned.1.call-start = ((), (), s32[]{:S(2)}) async-start(), calls=%async_computation.11 | async-start | bytes 18874368 | tf_op jit(solution)/shard_map/reduce_scatter | solution.py:93
  1107.7 177.4 %reduce-scatter.7.cloned.1.call-start = ((), (), s32[]{:S(2)}) async-start(), calls=%async_computation.9 | async-start | bytes 18874368 | tf_op jit(solution)/shard_map/reduce_scatter | solution.py:66
  1154.5 130.6 %copy-start.65 = (f32[1,2048]{1,0:T(1,128)S(1)}, f32[1,2048]{1,0:T(1,128)}, u32[]{:S(2)}) copy-start(f32[1,2048]{1,0:T(1,128)} %get-tuple-element.112) | copy-start | bytes 24580
  1154.5 130.6 %copy-start.74 = (f32[1,2048]{1,0:T(1,128)S(1)}, f32[1,2048]{1,0:T(1,128)}, u32[]{:S(2)}) copy-start(f32[1,2048]{1,0:T(1,128)} %copy-done.73) | copy-start | bytes 24580
  1154.5 130.6 %copy-start.76 = (f32[1,2048]{1,0:T(1,128)S(1)}, f32[1,2048]{1,0:T(1,128)}, u32[]{:S(2)}) copy-start(f32[1,2048]{1,0:T(1,128)} %copy-done.75) | copy-start | bytes 24580
  1154.6 130.6 %copy-start.82 = (f32[1,2048]{1,0:T(1,128)S(1)}, f32[1,2048]{1,0:T(1,128)}, u32[]{:S(2)}) copy-start(f32[1,2048]{1,0:T(1,128)} %get-tuple-element.117) | copy-start | bytes 24580
  1154.6 223.8 %all-gather.17.cloned.1.call-start = ((), (), s32[]{:S(2)}) async-start(), calls=%async_computation.12 | async-start | bytes 18874368 | tf_op jit(solution)/shard_map/all_gather | solution.py:84
  1296.6 592.5 %reduce-scatter.11.cloned.1.call-start = ((), (), s32[]{:S(2)}) async-start(), calls=%async_computation.13 | async-start | bytes 18874368 | tf_op jit(solution)/shard_map/reduce_scatter | solution.py:93
  1706.7 238.3 %all-reduce.19.cloned.1.call-start = ((), (), s32[]{:S(2)}) async-start(), calls=%async_computation.14 | async-start | bytes 139264 | tf_op jit(solution)/shard_map/psum | solution.py:96
  (97 other events, 1266.7 us)
Sparse Core Ops, SparseCore 0:
  25.8 84.3 all-gather.6
  111.9 21.4 all-gather.10
  135.0 21.5 all-gather.8
  355.5 87.4 reduce-scatter.4
  445.0 81.5 all-gather.14
  528.7 81.6 all-gather.12
  1107.9 87.4 reduce-scatter.8
  1197.7 87.3 reduce-scatter.6
  1296.7 81.5 all-gather.16
  1706.8 87.4 reduce-scatter.10
  1895.3 49.5 all-reduce.18
where the time goes:
time: 2060 us
  matrix products  702 us (34%)
  waiting for transfers between devices  519 us (25%)
  other arithmetic  509 us (25%)
  local copies, waits for them, and re-layouts  308 us (15%)
    reduce_scatter x2, waiting for transfers between devices, device_fn(): lax.psum_scatter(part_out.astype(jnp.bfloat16), 'tp', scatter_dimension=1...  157 us
    dot_general x6, matrix products, mix_heads(): jnp.einsum('bhqk,bkhe->bqhe', attn_probs, v_part, preferred_element_type=...  152 us
    all_gather x2, waiting for transfers between devices, device_fn(): lax.all_gather(gated_grad.astype(jnp.bfloat16), 'tp', axis=1, tiled=True)  138 us
    all_gather x2, waiting for transfers between devices, device_fn(): normed_full = lax.all_gather(normed, 'tp', axis=1, tiled=True)  136 us
    another operation x9, other arithmetic, device_fn(): jnp.stack([block_grads[block_idx][entry_idx] for block_idx in range(num_b...  123 us
    dot_general x6, matrix products, mix_heads(): jnp.einsum('bqhe,bkhe->bhqk', q_rot, k_rot, preferred_element_type=jnp.fl...  118 us
    unnamed x236, local copies, waits for them, and re-layouts  93.4 us
    mul x2, other arithmetic, mix_heads(): jnp.einsum('bqhe,bkhe->bhqk', q_rot, k_rot, preferred_element_type=jnp.fl...  87.4 us
  transfers between devices with their start and end apart: 11, of which 8 were waited for; matrix products, arithmetic and copies ran while one was open for 20% of the time, Pallas kernels for 0%

commit v1 on v0

v1 whole, which is shorter than its diff:
```python
import functools
import jax
import jax.numpy as jnp
from jax import lax
from jax.sharding import PartitionSpec as P
from jax.experimental import pallas as pl
from jax.experimental.pallas import tpu as pltpu

NORM_EPS = 1e-6
NUM_CHUNKS = 2
TILE = 512
F32 = jnp.float32
BF16 = jnp.bfloat16
LANES = 128
GELU_A = 0.7978845608028654
GELU_B = 0.044715


def call(body, **kw):
    flops = kw.pop("flops")
    nbytes = kw.pop("nbytes")
    kw["cost_estimate"] = pl.CostEstimate(flops=int(flops), bytes_accessed=int(nbytes), transcendentals=0)
    kw["compiler_params"] = pltpu.CompilerParams(dimension_semantics=("arbitrary",), vmem_limit_bytes=60 * 1024 * 1024)
    return pl.pallas_call(body, **kw)


def full(shape):
    return pl.BlockSpec(shape, lambda i: (0,) * len(shape))


def rows(tile, cols):
    return pl.BlockSpec((tile, cols), lambda i: (i, 0))


def dot(a, b, dims=((1,), (0,))):
    return lax.dot_general(a, b, (dims, ((), ())), preferred_element_type=F32)


def as_row(col):
    return jnp.broadcast_to(col, (col.shape[0], LANES)).T[:8]


def inproj_body(h_ref, w_ref, b_ref, qs_ref, ks_ref, cs_ref, q_ref, k_ref, v_ref, j_ref, yqk_ref, u_ref):
    hd = q_ref.shape[1]
    half = hd // 2
    h = h_ref[...]
    cos = cs_ref[:, :half]
    sin = cs_ref[:, half:]
    for part, (s_ref, o_ref, post) in enumerate(((qs_ref, q_ref, hd ** -0.5), (ks_ref, k_ref, None))):
        lo = part * hd
        y = dot(h, w_ref[:, lo:lo + hd]) + b_ref[:, lo:lo + hd]
        yqk_ref[:, lo:lo + hd] = y
        inv = lax.rsqrt(jnp.mean(y * y, axis=-1, keepdims=True) + NORM_EPS)
        t = y * inv * s_ref[...]
        ta, tb = t[:, :half], t[:, half:]
        ra = ta * cos - tb * sin
        rb = ta * sin + tb * cos
        ra = ra.astype(BF16)
        rb = rb.astype(BF16)
        if post is not None:
            ra = ra * BF16(post)
            rb = rb * BF16(post)
        o_ref[:, :half] = ra
        o_ref[:, half:] = rb
    v_ref[...] = (dot(h, w_ref[:, 2 * hd:3 * hd]) + b_ref[:, 2 * hd:3 * hd]).astype(BF16)
    j_ref[:, :hd] = jnp.zeros((h.shape[0], hd), BF16)
    mlp = u_ref.shape[1]
    for lo in range(0, mlp, 256):
        c0 = 3 * hd + lo
        u = dot(h, w_ref[:, c0:c0 + 256]) + b_ref[:, c0:c0 + 256]
        u_ref[:, lo:lo + 256] = u
        g = 0.5 * u * (1.0 + jnp.tanh(GELU_A * (u + GELU_B * (u * u * u))))
        j_ref[:, hd + lo:hd + lo + 256] = g.astype(BF16)


def inproj(h, w, b, qs, ks, cs):
    s, d = h.shape
    n = w.shape[1]
    hd = qs.shape[1]
    mlp = n - 3 * hd
    tile = min(TILE, s)
    return call(
        inproj_body,
        grid=(s // tile,),
        in_specs=[rows(tile, d), full((d, n)), full((1, n)), full((1, hd)), full((1, hd)), rows(tile, hd)],
        out_specs=[rows(tile, hd)] * 3 + [rows(tile, hd + mlp), rows(tile, 2 * hd), rows(tile, mlp)],
        out_shape=[jax.ShapeDtypeStruct((s, hd), BF16)] * 3
        + [jax.ShapeDtypeStruct((s, hd + mlp), BF16), jax.ShapeDtypeStruct((s, 2 * hd), F32), jax.ShapeDtypeStruct((s, mlp), F32)],
        flops=2 * s * d * n,
        nbytes=s * d * 2 + d * n * 2 + s * n * 6,
        name="inproj",
    )(h, w, b, qs, ks, cs)


def attn_body(nc, bk, q_ref, *refs):
    k_refs, v_refs, _, o_ref, lse_ref = refs[:nc], refs[nc:2 * nc], refs[2 * nc], refs[2 * nc + 1], refs[2 * nc + 2]
    q = q_ref[...]
    pieces = [(c, lo) for c in range(nc) for lo in range(0, k_refs[0].shape[0], bk)]

    def score(idx):
        c, lo = pieces[idx]
        return dot(q, k_refs[c][lo:lo + bk, :], ((1,), (1,)))

    m = l = acc = None
    s_next = score(0)
    for idx, (c, lo) in enumerate(pieces):
        s = s_next
        if idx + 1 < len(pieces):
            s_next = score(idx + 1)
        top = jnp.max(s, axis=-1, keepdims=True)
        m_new = top if m is None else jnp.maximum(m, top)
        p = jnp.exp(s - m_new)
        psum = jnp.sum(p, axis=-1, keepdims=True)
        pv = dot(p.astype(BF16), v_refs[c][lo:lo + bk, :])
        if m is None:
            l, acc = psum, pv
        else:
            alpha = jnp.exp(m - m_new)
            l = l * alpha + psum
            acc = acc * alpha + pv
        m = m_new
    o_ref[...] = (acc / l).astype(BF16)
    lse_ref[...] = as_row(m + jnp.log(l))


def attention(q, ks, vs, joined, bq=512, bk=1024):
    s, hd = q.shape
    nc = len(ks)
    bq = min(bq, s)
    bk = min(bk, s)
    kv = [full((s, hd))] * (2 * nc)
    return call(
        functools.partial(attn_body, nc, bk),
        grid=(s // bq,),
        in_specs=[rows(bq, hd)] + kv + [pl.BlockSpec(memory_space=pl.ANY)],
        out_specs=[rows(bq, hd), pl.BlockSpec((8, bq), lambda i: (0, i))],
        out_shape=[jax.ShapeDtypeStruct(joined.shape, BF16), jax.ShapeDtypeStruct((8, s), F32)],
        input_output_aliases={1 + 2 * nc: 0},
        flops=4 * s * s * nc * hd,
        nbytes=2 * s * hd * (2 + 2 * nc),
        name="attn_fwd",
    )(q, *ks, *vs, joined)


def outproj_bwd_body(db_ref, w_ref, u_ref, o_ref, do_ref, delta_ref, dp_ref, gb_ref):
    hd = do_ref.shape[1]
    mlp = u_ref.shape[1]
    db = db_ref[...]
    do = dot(db, w_ref[:, :hd]).astype(BF16)
    do_ref[...] = do
    delta_ref[...] = as_row(jnp.sum(do.astype(F32) * o_ref[...].astype(F32), axis=-1, keepdims=True))

    @pl.when(pl.program_id(0) == 0)
    def _():
        gb_ref[...] = jnp.zeros_like(gb_ref)

    for lo in range(0, mlp, 256):
        dm = dot(db, w_ref[:, hd + lo:hd + lo + 256]).astype(BF16).astype(F32)
        u = u_ref[:, lo:lo + 256]
        u2 = u * u
        t = jnp.tanh(GELU_A * (u + GELU_B * (u2 * u)))
        grad = 0.5 * (1.0 + t) + 0.5 * u * (1.0 - t * t) * (GELU_A * (1.0 + 3.0 * GELU_B * u2))
        du = dm * grad
        gb_ref[:, lo:lo + 256] += jnp.sum(du, axis=0, keepdims=True)
        dp_ref[:, 3 * hd + lo:3 * hd + lo + 256] = du.astype(BF16)
    dp_ref[:, :3 * hd] = jnp.zeros((db.shape[0], 3 * hd), BF16)


def outproj_bwd(db, wt, u, joined):
    s, d = db.shape
    n = wt.shape[1]
    mlp = u.shape[1]
    hd = n - mlp
    tile = min(TILE, s)
    return call(
        outproj_bwd_body,
        grid=(s // tile,),
        in_specs=[rows(tile, d), full((d, n)), rows(tile, mlp), rows(tile, hd)],
        out_specs=[rows(tile, hd), pl.BlockSpec((8, tile), lambda i: (0, i)), rows(tile, 3 * hd + mlp), full((1, mlp))],
        out_shape=[jax.ShapeDtypeStruct((s, hd), BF16), jax.ShapeDtypeStruct((8, s), F32),
                   jax.ShapeDtypeStruct((s, 3 * hd + mlp), BF16), jax.ShapeDtypeStruct((1, mlp), F32)],
        flops=2 * s * d * n,
        nbytes=s * d * 2 + d * n * 2 + s * mlp * 4 + s * n * 3,
        name="outproj_bwd",
    )(db, wt, u, joined)


def attn_bwd_body(nc, bq, k_ref, v_ref, *refs):
    q_refs, do_refs, lse_refs, dl_refs = (refs[j * nc:(j + 1) * nc] for j in range(4))
    dq_refs, dk_ref, dv_ref = refs[4 * nc:5 * nc], refs[5 * nc], refs[5 * nc + 1]
    k = k_ref[...]
    v = v_ref[...]
    first = pl.program_id(0) == 0

    @pl.when(first)
    def _():
        for c in range(nc):
            dq_refs[c][...] = jnp.zeros_like(dq_refs[c])

    dk_ref[...] = jnp.zeros_like(dk_ref)
    dv_ref[...] = jnp.zeros_like(dv_ref)
    for c in range(nc):
        @pl.loop(0, q_refs[c].shape[0] // bq)
        def _(t, c=c):
            at = pl.ds(pl.multiple_of(t * bq, bq), bq)
            q = q_refs[c][at, :]
            do = do_refs[c][at, :]
            s = dot(k, q, ((1,), (1,)))
            dp = dot(v, do, ((1,), (1,)))
            p = jnp.exp(s - lse_refs[c][:1, at])
            dv_ref[...] += dot(p.astype(BF16), do)
            ds = (p * (dp - dl_refs[c][:1, at])).astype(BF16)
            dk_ref[...] += dot(ds, q)
            dq_refs[c][at, :] += dot(ds, k, ((0,), (0,)))


def attention_bwd(k, v, qs, dos, lses, deltas, bq=512, bk=512):
    s, hd = k.shape
    nc = len(qs)
    bq = min(bq, s)
    bk = min(bk, s)
    return call(
        functools.partial(attn_bwd_body, nc, bq),
        grid=(s // bk,),
        in_specs=[rows(bk, hd)] * 2 + [full((s, hd))] * (2 * nc) + [full((8, s))] * (2 * nc),
        out_specs=[full((s, hd))] * nc + [rows(bk, hd)] * 2,
        out_shape=[jax.ShapeDtypeStruct((s, hd), F32)] * (nc + 2),
        flops=10 * s * s * nc * hd,
        nbytes=2 * s * hd * (4 + 4 * nc),
        name="attn_bwd",
    )(k, v, *qs, *dos, *lses, *deltas)


def qk_bwd_body(nc, y_ref, cs_ref, qs_ref, ks_ref, *refs):
    dq_refs, dk_ref, dv_ref, _ = refs[:nc], refs[nc], refs[nc + 1], refs[nc + 2]
    dp_ref, gb_ref, gs_ref = refs[nc + 3:]
    hd = dk_ref.shape[1]
    half = hd // 2

    @pl.when(pl.program_id(0) == 0)
    def _():
        gb_ref[...] = jnp.zeros_like(gb_ref)
        gs_ref[...] = jnp.zeros_like(gs_ref)

    cos = cs_ref[:, :half]
    sin = cs_ref[:, half:]
    dq = dq_refs[0][...]
    for r in dq_refs[1:]:
        dq = dq + r[...]
    for part, (g, s_ref) in enumerate(((dq * hd ** -0.5, qs_ref), (dk_ref[...], ks_ref))):
        lo = part * hd
        y = y_ref[:, lo:lo + hd]
        inv = lax.rsqrt(jnp.mean(y * y, axis=-1, keepdims=True) + NORM_EPS)
        n = y * inv
        ga, gb = g[:, :half], g[:, half:]
        dt = jnp.concatenate([ga * cos + gb * sin, gb * cos - ga * sin], axis=1)
        gs_ref[:, lo:lo + hd] += jnp.sum(dt * n, axis=0, keepdims=True)
        dn = dt * s_ref[...]
        dy = inv * (dn - n * jnp.mean(dn * n, axis=-1, keepdims=True))
        gb_ref[:, lo:lo + hd] += jnp.sum(dy, axis=0, keepdims=True)
        dp_ref[:, lo:lo + hd] = dy.astype(BF16)
    dv = dv_ref[...]
    gb_ref[:, 2 * hd:] += jnp.sum(dv, axis=0, keepdims=True)
    dp_ref[:, 2 * hd:] = dv.astype(BF16)


def qk_bwd(yqk, cs, qs, ks, dqs, dk, dv, dproj):
    s, hd = dk.shape
    nc = len(dqs)
    tile = min(TILE, s)
    return call(
        functools.partial(qk_bwd_body, nc),
        grid=(s // tile,),
        in_specs=[rows(tile, 2 * hd), rows(tile, hd), full((1, hd)), full((1, hd))] + [rows(tile, hd)] * (nc + 2)
        + [pl.BlockSpec(memory_space=pl.ANY)],
        out_specs=[rows(tile, 3 * hd), full((1, 3 * hd)), full((1, 2 * hd))],
        out_shape=[jax.ShapeDtypeStruct(dproj.shape, BF16), jax.ShapeDtypeStruct((1, 3 * hd), F32), jax.ShapeDtypeStruct((1, 2 * hd), F32)],
        input_output_aliases={6 + nc: 0},
        flops=100 * s * hd,
        nbytes=s * hd * 4 * (6 + nc),
        name="qk_bwd",
    )(yqk, cs, qs, ks, *dqs, dk, dv, dproj)


def wgrad_body(nc, unsplit, *refs):
    a_refs, b_refs = refs[:nc], refs[nc:2 * nc]
    out_ref = refs[-1]
    acc = None
    for a, b in zip(a_refs, b_refs):
        part = dot(a[...], b[...], ((0,), (0,)))
        acc = part if acc is None else acc + part
    g = acc.astype(BF16)
    if unsplit:
        sel = refs[2 * nc][...]
        hd = sel.shape[0]
        for lo in (0, hd):
            out_ref[0, :, lo:lo + hd] = dot(g[:, lo:lo + hd], sel, ((1,), (1,))).astype(BF16)
        out_ref[0, :, 2 * hd:] = g[:, 2 * hd:]
    else:
        out_ref[0] = g


def wgrad(a_list, b_list, sel, block, num_blocks, prev, tile=256):
    nc = len(a_list)
    s, m = a_list[0].shape
    n = b_list[0].shape[1]
    args = list(a_list) + list(b_list)
    specs = [pl.BlockSpec((s, tile), lambda i: (0, i))] * nc
    specs += [pl.BlockSpec((s, n), lambda i: (0, 0), pipeline_mode=pl.Buffered(1))] * nc
    if sel is not None:
        args.append(sel)
        specs.append(full(sel.shape))
    alias = {}
    if prev is not None:
        alias = {len(args): 0}
        args.append(prev)
        specs.append(pl.BlockSpec(memory_space=pl.ANY))
    return call(
        functools.partial(wgrad_body, nc, sel is not None),
        grid=(m // tile,),
        in_specs=specs,
        out_specs=pl.BlockSpec((1, tile, n), lambda i: (block, i, 0)),
        out_shape=jax.ShapeDtypeStruct((num_blocks, m, n), BF16),
        input_output_aliases=alias,
        flops=2 * s * nc * m * n,
        nbytes=2 * (s * nc * (m + n) + m * n),
        name="wgrad_in" if sel is not None else "wgrad_out",
    )(*args)


def outer_body(col_ref, row_ref, *refs):
    refs[-1][0] = col_ref[...] * row_ref[...]


def outer(col, row, block, num_blocks, prev, tile=256):
    m, n = col.shape[0], row.shape[1]
    args = [col, row]
    specs = [rows(tile, 1), full((1, n))]
    alias = {}
    if prev is not None:
        alias = {2: 0}
        args.append(prev)
        specs.append(pl.BlockSpec(memory_space=pl.ANY))
    return call(
        outer_body,
        grid=(m // tile,),
        in_specs=specs,
        out_specs=pl.BlockSpec((1, tile, n), lambda i: (block, i, 0)),
        out_shape=jax.ShapeDtypeStruct((num_blocks, m, n), F32),
        input_output_aliases=alias,
        flops=50 * m * n,
        nbytes=4 * m * n,
        name="outer",
    )(*args)


def vec_sum_body(n, v_ref, o_ref, recv, send_sem, recv_sem):
    me = lax.axis_index("tp")
    barrier = pltpu.get_barrier_semaphore()
    for d in range(1, n):
        pl.semaphore_signal(barrier, inc=1, device_id={"tp": lax.rem(me + d, n)}, device_id_type=pl.DeviceIdType.MESH)
    pl.semaphore_wait(barrier, n - 1)
    sends = []
    for d in range(1, n):
        cp = pltpu.make_async_remote_copy(
            src_ref=v_ref, dst_ref=recv.at[me], send_sem=send_sem.at[d], recv_sem=recv_sem.at[me],
            device_id={"tp": lax.rem(me + d, n)}, device_id_type=pl.DeviceIdType.MESH)
        cp.start()
        sends.append(cp)
    recv[me] = v_ref[...]
    for d in range(1, n):
        src = lax.rem(me + d, n)
        pltpu.make_async_remote_copy(
            src_ref=v_ref, dst_ref=recv.at[src], send_sem=send_sem.at[d], recv_sem=recv_sem.at[src],
            device_id={"tp": src}, device_id_type=pl.DeviceIdType.MESH).wait_recv()
    total = recv[0]
    for d in range(1, n):
        total = total + recv[d]
    o_ref[...] = total
    for cp in sends:
        cp.wait_send()


def vec_sum(vec, n, cid):
    w = vec.shape[1]
    r = -(-w // LANES)
    r = -(-r // 8) * 8
    packed = jnp.pad(vec, ((0, 0), (0, r * LANES - w))).reshape(r, LANES)
    out = pl.pallas_call(
        functools.partial(vec_sum_body, n),
        in_specs=[pl.BlockSpec(memory_space=pltpu.VMEM)],
        out_specs=pl.BlockSpec(memory_space=pltpu.VMEM),
        out_shape=jax.ShapeDtypeStruct((r, LANES), F32),
        scratch_shapes=[pltpu.VMEM((n, r, LANES), F32), pltpu.SemaphoreType.DMA((n,)), pltpu.SemaphoreType.DMA((n,))],
        compiler_params=pltpu.CompilerParams(collective_id=cid, has_side_effects=True),
        cost_estimate=pl.CostEstimate(flops=10 ** 8, bytes_accessed=10 ** 6, transcendentals=0),
        name="vec_sum",
    )(packed)
    return out.reshape(1, r * LANES)[:, :w]


def layer_modulate(x_f32, mod_shift, mod_scale):
    row_mean = jnp.mean(x_f32, axis=-1, keepdims=True)
    centered = x_f32 - row_mean
    row_var = jnp.mean(centered * centered, axis=-1, keepdims=True)
    normed = centered * lax.rsqrt(row_var + NORM_EPS)
    return (normed * (1.0 + mod_scale) + mod_shift).astype(BF16)


def split_pairs(cols):
    src = lax.broadcasted_iota(jnp.int32, (cols, cols), 0)
    dst = lax.broadcasted_iota(jnp.int32, (cols, cols), 1)
    return (dst == src // 2 + (src % 2) * (cols // 2)).astype(BF16)


def unpair(vec):
    half = vec.shape[-1] // 2
    return jnp.stack([vec[..., :half], vec[..., half:]], axis=-1).reshape(vec.shape)


def pair(vec):
    return jnp.concatenate([vec[..., 0::2], vec[..., 1::2]], axis=-1)


def solution(mesh):
    act_spec = P("dp", "tp", None)
    in_specs = (act_spec, P("dp", None), P("tp", None), P("tp", None), P(None, None, None), P(None, None), P(None, None, "tp", None), P(None, "tp", None), P(None, None), P(None, None), P(None, "tp", None, None), P(None, None), act_spec)
    out_specs = (act_spec, act_spec, P("dp", None, None), P("dp", None), P("dp", None, "tp", None), P("dp", "tp", None), P("dp", None), P("dp", None), P("dp", "tp", None, None), P("dp", None))

    def device_fn(x_in, cond_vec, rope_cos, rope_sin, w_mod, b_mod, w_in, b_in, q_scale, k_scale, w_out, b_out, d_out):
        nb = w_in.shape[0]
        hd = q_scale.shape[1]
        nc = NUM_CHUNKS
        x_cur = x_in[0]
        ts, dim = x_cur.shape
        cw = ts // nc

        def gather(t):
            return [lax.all_gather(t[c * cw:(c + 1) * cw], "tp", axis=0, tiled=True) for c in range(nc)]

        def scatter(parts):
            return [lax.psum_scatter(p, "tp", scatter_dimension=0, tiled=True) for p in parts]

        silu_vec = jax.nn.silu(cond_vec.astype(F32)).astype(BF16)
        silu_col = silu_vec.astype(F32).reshape(-1, 1)
        n_tp = mesh.shape["tp"]
        sel = split_pairs(hd)
        cs_local = jnp.concatenate([rope_cos, rope_sin], axis=1).reshape(nc, cw, hd)
        cs = lax.all_gather(cs_local, "tp", axis=1, tiled=True)
        w_perm, b_perm, w_o, w_ot, qsc, ksc, mods = [], [], [], [], [], [], []

        def prepare(l, silu_vec, sel):
            mods.append(jnp.split(jnp.dot(silu_vec, w_mod[l], preferred_element_type=F32) + b_mod[l].astype(F32), 3, axis=-1))
            wl = w_in[l, :, 0, :]
            wq = jnp.dot(wl[:, :hd], sel, preferred_element_type=F32).astype(BF16)
            wk = jnp.dot(wl[:, hd:2 * hd], sel, preferred_element_type=F32).astype(BF16)
            w_perm.append(jnp.concatenate([wq, wk, wl[:, 2 * hd:]], axis=1))
            bl = b_in[l].astype(F32)
            b_perm.append(jnp.concatenate([pair(bl[:, :hd]), pair(bl[:, hd:2 * hd]), bl[:, 2 * hd:]], axis=1))
            w_o.append(w_out[l, 0])
            w_ot.append(w_out[l, 0].T)
            qsc.append(pair(q_scale[l:l + 1].astype(F32)))
            ksc.append(pair(k_scale[l:l + 1].astype(F32)))

        prepare(0, silu_vec, sel)
        saved = []
        for l in range(nb):
            shift, scale, gate = mods[l]
            x_f32 = x_cur.astype(F32)
            h = layer_modulate(x_f32, shift, scale)
            hf = gather(h)
            if l == nb - 1:
                gated_last = (d_out[0].astype(F32) * gate).astype(BF16)
                gated_last, hf[-1] = lax.optimization_barrier((gated_last, hf[-1]))
                db_last = gather(gated_last)
            proj = [inproj(hf[c], w_perm[l], b_perm[l], qsc[l], ksc[l], cs[c]) for c in range(nc)]
            if l + 1 < nb:
                prepare(l + 1, *lax.optimization_barrier((silu_vec, sel, proj[0][0]))[:2])
            qs, ks, vs, js, yqk, us = map(list, zip(*proj))
            lses, zs = [], []
            for c in range(nc):
                js[c], lse = attention(qs[c], ks, vs, js[c])
                lses.append(lse)
                zs.append(jnp.dot(js[c], w_o[l], preferred_element_type=F32).astype(BF16))
            if l == nb - 1:
                db_last[0], zs = lax.optimization_barrier((db_last[0], zs))
            mixed = jnp.concatenate(scatter(zs), axis=0)
            if l < nb - 1:
                branch = mixed.astype(F32) + b_out[l].astype(F32)
                x_cur = (x_f32 + gate * branch).astype(BF16)
            saved.append((x_f32, hf, qs, ks, vs, js, yqk, us, lses, mixed))

        grad_cur = d_out[0]
        grads = {}
        g_win = g_wout = g_wmod = None
        for l in reversed(range(nb)):
            x_f32, hf, qs, ks, vs, js, yqk, us, lses, mixed = saved[l]
            shift, scale, gate = mods[l]
            grad_f32 = grad_cur.astype(F32)
            gated = grad_f32 * gate
            d_bout = jnp.sum(gated, axis=0)
            db = db_last if l == nb - 1 else gather(gated.astype(BF16))
            if l < nb - 1:
                db[0], g_win, g_wout = lax.optimization_barrier((db[0], g_win, g_wout))
            back = [outproj_bwd(db[c], w_ot[l], us[c], js[c]) for c in range(nc)]
            dos, deltas, dprojs, gbu = map(list, zip(*back))
            dqs = [[] for _ in range(nc)]
            dks, dvs = [], []
            for c in range(nc):
                res = attention_bwd(ks[c], vs[c], qs, dos, lses, deltas)
                for e in range(nc):
                    dqs[e].append(res[e])
                dks.append(res[nc])
                dvs.append(res[nc + 1])
            gb3, gsc, dns = [], [], []
            for c in range(nc):
                dprojs[c], b3, s2 = qk_bwd(yqk[c], cs[c], qsc[l], ksc[l], dqs[c], dks[c], dvs[c], dprojs[c])
                gb3.append(b3)
                gsc.append(s2)
                dns.append(lax.dot_general(dprojs[c], w_perm[l], (((1,), (1,)), ((), ())), preferred_element_type=F32).astype(BF16))
            d_normed = scatter(dns)
            g_wout = wgrad(js, db, None, l, nb, g_wout)
            g_win = wgrad(hf, dprojs, sel, l, nb, g_win)
            d_normed, mixed, g_win = lax.optimization_barrier((d_normed, mixed, g_win))
            d_normed = jnp.concatenate(d_normed, axis=0)
            branch = mixed.astype(F32) + b_out[l].astype(F32)
            if l == nb - 1:
                x_out = (x_f32 + gate * branch).astype(BF16)
            gb3, gbu, gsc = sum(gb3), sum(gbu), sum(gsc)
            g_bin = jnp.concatenate([unpair(gb3[:, :hd]), unpair(gb3[:, hd:2 * hd]), gb3[:, 2 * hd:], gbu], axis=1)
            d_gate = jnp.sum(grad_f32 * branch, axis=0, keepdims=True)
            unused, norm_pull = jax.vjp(layer_modulate, x_f32, shift, scale)
            d_xnorm, d_shift, d_scale = norm_pull(d_normed)
            summed = vec_sum(jnp.concatenate([d_shift, d_scale, d_gate, d_bout[None], gsc], axis=1), n_tp, l)
            d_mod = summed[:, :3 * dim]
            g_wmod = outer(silu_col, d_mod, l, nb, g_wmod)
            d_qs = unpair(summed[0, 4 * dim:4 * dim + hd])
            d_ks = unpair(summed[0, 4 * dim + hd:])
            grads[l] = (d_mod[0], g_bin, d_qs, d_ks, summed[0, 3 * dim:4 * dim])
            grad_cur = (grad_f32 + d_xnorm).astype(BF16)
        g_bmod, g_bin, g_qs, g_ks, g_bout = (jnp.stack([grads[l][e] for l in range(nb)]) for e in range(5))
        return (x_out[None], grad_cur[None], g_wmod, g_bmod, g_win[:, :, None, :], g_bin, g_qs, g_ks, g_wout[:, None], g_bout)

    return jax.shard_map(device_fn, mesh=mesh, in_specs=in_specs, out_specs=out_specs, check_vma=False)
```

time: 2060 us -> 1170 us (0.57)
  Pallas kernels: 0 us -> 615 us
  matrix products: 702 us -> 176 us
  other arithmetic: 509 us -> 56.3 us
  waiting for transfers between devices: 519 us -> 229 us
  local copies, waits for them, and re-layouts: 308 us -> 70.2 us
    pallas_call x0 -> x28, Pallas kernels: none -> 615 us  [the longest x4 140 us: wgrad(): call(functools.partial(wgrad_body, nc, sel is not None), grid=(m // tile,...]
    dot_general x26 -> x14, matrix products: 702 us -> 176 us  [the longest x4 83.2 us: device_fn(): lax.dot_general(dprojs[c], w_perm[l], (((1,), (1,)), ((), ())), preferred...]
    another operation x16 -> x15, other arithmetic: 141 us -> 3.16 us  [the longest x7 3.09 us: device_fn(): jnp.stack([grads[l][e] for l in range(nb)])]
    all_gather x6 -> x9, waiting for transfers between devices: 274 us -> 146 us  [the longest x8 146 us: gather(): lax.all_gather(t[c * cw:(c + 1) * cw], 'tp', axis=0, tiled=True)]
    reduce_scatter x4 -> x8, waiting for transfers between devices: 198 us -> 79.4 us  [scatter(): lax.psum_scatter(p, 'tp', scatter_dimension=0, tiled=True)]
    mul x4 -> x0, other arithmetic: 105 us -> none  [the longest x2 87.4 us: mix_heads(): jnp.einsum('bqhe,bkhe->bhqk', q_rot, k_rot, preferred_element_type=jnp.fl...]
    reduce_sum x13 -> x6, other arithmetic: 109 us -> 19.9 us  [the longest x2 7.96 us: device_fn(): d_bout = jnp.sum(gated, axis=0)]
    unnamed x236 -> x181, local copies, waits for them, and re-layouts: 93.4 us -> 21.3 us
  transfers between devices with their start and end apart: 11 -> 17, of which waited for: 8 -> 9; matrix products, arithmetic and copies ran while one was open for 20% -> 19% of each run, Pallas kernels for 0% -> 39%
where the time goes in v1:
time: 1170 us; the launch traced here: 1160 us
  Pallas kernels  615 us (53%)
  waiting for transfers between devices  229 us (20%)
  matrix products  176 us (15%)
  local copies, waits for them, and re-layouts  70.2 us (6%)
  other arithmetic  56.3 us (5%)
  between operations  15.6 us (1%)
    all_gather x8, waiting for transfers between devices, gather(): lax.all_gather(t[c * cw:(c + 1) * cw], 'tp', axis=0, tiled=True)  146 us
    pallas_call x4, Pallas kernels, wgrad(): call(functools.partial(wgrad_body, nc, sel is not None), grid=(m // tile,...  140 us
    pallas_call x4, Pallas kernels, attention_bwd(): call(functools.partial(attn_bwd_body, nc, bq), grid=(s // bk,), in_specs=...  139 us
    pallas_call x4, Pallas kernels, inproj(): call(inproj_body, grid=(s // tile,), in_specs=[rows(tile, d), full((d, n)...  94.7 us
    pallas_call x4, Pallas kernels, outproj_bwd(): call(outproj_bwd_body, grid=(s // tile,), in_specs=[rows(tile, d), full((...  91.3 us
    dot_general x4, matrix products, device_fn(): lax.dot_general(dprojs[c], w_perm[l], (((1,), (1,)), ((), ())), preferred...  83.2 us
    reduce_scatter x8, waiting for transfers between devices, scatter(): lax.psum_scatter(p, 'tp', scatter_dimension=0, tiled=True)  79.4 us
    dot_general x4, matrix products, device_fn(): zs.append(jnp.dot(js[c], w_o[l], preferred_element_type=F32).astype(BF16))  66.4 us
  transfers between devices with their start and end apart: 17, of which 9 were waited for; matrix products, arithmetic and copies ran while one was open for 19% of the time, Pallas kernels for 39%

profile of v1, /device:TPU:113, one launch (start us, length us, event | category | flops | bytes accessed | tf_op | source)
XLA Modules:
  0.0 1164.1 jit_solution(4748373843288902243)
XLA Ops:
  48.5 40.3 %all-gather.14.cloned.1.call-done.h_ref.refs_1_ = bf16[2048,2048]{1,0:T(8,128)(2,1)} async-done(((bf16[256,2048]{1,0:T(8,128)(2,1)}), bf16[2048,2048]{1,0:T(8,128)(2,1)}) %all-gather.14.cloned.1.call-update) | async-done | bytes 8388624 | tf_op jit(solution)/shard_map/all_gather | solution.py:439
  88.8 23.7 %inproj.5 = (bf16[2048,256]{1,0:T(8,128)(2,1)}, bf16[2048,256]{1,0:T(8,128)(2,1)}, bf16[2048,256]{1,0:T(8,128)(2,1)}, bf16[2048,1280]{1,0:T(8,128)(2,1)}, f32[2048,512]{1,0:T(8,128)}, /*index=5*/f32[2048,1024]{1,0:T(8,128)}) custom-call(bf16[2048,2048]{1,0:T(8,128)(2,1)} %all-gather.14.cloned.1.call-done.h_ref.refs_1_, ...), custom_call_target="tpu_custom_call" | custom-call | flops 15032385536 | bytes 37748736 | tf_op jit(solution)/shard_map/inproj/pallas_call | solution.py:82
  112.5 24.2 %all-gather.10.cloned.1.call-done.h_ref.refs_0_ = bf16[2048,2048]{1,0:T(8,128)(2,1)} async-done(((bf16[256,2048]{1,0:T(8,128)(2,1)}), bf16[2048,2048]{1,0:T(8,128)(2,1)}) %all-gather.10.cloned.1.call-update) | async-done | bytes 8388624 | tf_op jit(solution)/shard_map/all_gather | solution.py:439
  136.7 23.7 %inproj.4 = (bf16[2048,256]{1,0:T(8,128)(2,1)}, bf16[2048,256]{1,0:T(8,128)(2,1)}, bf16[2048,256]{1,0:T(8,128)(2,1)}, bf16[2048,1280]{1,0:T(8,128)(2,1)}, f32[2048,512]{1,0:T(8,128)}, /*index=5*/f32[2048,1024]{1,0:T(8,128)}) custom-call(bf16[2048,2048]{1,0:T(8,128)(2,1)} %all-gather.10.cloned.1.call-done.h_ref.refs_0_, ...), custom_call_target="tpu_custom_call" | custom-call | flops 15032385536 | bytes 37748736 | tf_op jit(solution)/shard_map/inproj/pallas_call | solution.py:82
  243.0 48.5 %reduce-scatter.11.cloned.1.call-done = bf16[256,2048]{1,0:T(8,128)(2,1)} async-done(((bf16[2048,2048]{1,0:T(8,128)(2,1)}), bf16[256,2048]{1,0:T(8,128)(2,1)}) %reduce-scatter.11.cloned.1.call-update) | async-done | bytes 1048592 | tf_op jit(solution)/shard_map/reduce_scatter | solution.py:442
  302.4 43.4 %all-gather.18.cloned.1.call-done.h_ref.refs_1_ = bf16[2048,2048]{1,0:T(8,128)(2,1)} async-done(((bf16[256,2048]{1,0:T(8,128)(2,1)}), bf16[2048,2048]{1,0:T(8,128)(2,1)}) %all-gather.18.cloned.1.call-update) | async-done | bytes 8388624 | tf_op jit(solution)/shard_map/all_gather | solution.py:439
  363.7 23.7 %inproj.7 = (bf16[2048,256]{1,0:T(8,128)(2,1)}, bf16[2048,256]{1,0:T(8,128)(2,1)}, bf16[2048,256]{1,0:T(8,128)(2,1)}, bf16[2048,1280]{1,0:T(8,128)(2,1)}, f32[2048,512]{1,0:T(8,128)}, /*index=5*/f32[2048,1024]{1,0:T(8,128)}) custom-call(bf16[2048,2048]{1,0:T(8,128)(2,1)} %all-gather.18.cloned.1.call-done.h_ref.refs_1_, ...), custom_call_target="tpu_custom_call" | custom-call | flops 15032385536 | bytes 37748736 | tf_op jit(solution)/shard_map/inproj/pallas_call | solution.py:82
  393.7 23.7 %inproj.6 = (bf16[2048,256]{1,0:T(8,128)(2,1)}, bf16[2048,256]{1,0:T(8,128)(2,1)}, bf16[2048,256]{1,0:T(8,128)(2,1)}, bf16[2048,1280]{1,0:T(8,128)(2,1)}, f32[2048,512]{1,0:T(8,128)}, /*index=5*/f32[2048,1024]{1,0:T(8,128)}) custom-call(bf16[2048,2048]{1,0:T(8,128)(2,1)} %all-gather.16.cloned.1.call-done.h_ref.refs_0_, ...), custom_call_target="tpu_custom_call" | custom-call | flops 15032385536 | bytes 37748736 | tf_op jit(solution)/shard_map/inproj/pallas_call | solution.py:82
  501.0 22.8 %outproj_bwd.4 = (bf16[2048,256]{1,0:T(8,128)(2,1)}, f32[8,2048]{1,0:T(8,128)}, bf16[2048,1792]{1,0:T(8,128)(2,1)}, f32[1,1024]{1,0:T(1,128)}) custom-call(bf16[2048,2048]{1,0:T(8,128)(2,1)} %all-gather.20.cloned.1.call-done.db_ref.refs_2_, bf16[2048,1280]{1,0:T(8,128)(2,1)} %bitcast.200, f32[2048,1024]{1,0:T(8,128)} %get-tuple-element.130.u_ref, ...), custom_call_target="tpu_custom_call" | custom-call | flops 10737418240 | bytes 29884416 | tf_op jit(solution)/shard_map/outproj_bwd/pallas_call | solution.py:175
  523.8 22.9 %outproj_bwd.5 = (bf16[2048,256]{1,0:T(8,128)(2,1)}, f32[8,2048]{1,0:T(8,128)}, bf16[2048,1792]{1,0:T(8,128)(2,1)}, f32[1,1024]{1,0:T(1,128)}) custom-call(bf16[2048,2048]{1,0:T(8,128)(2,1)} %all-gather.22.cloned.1.call-done.db_ref.refs_3_, bf16[2048,1280]{1,0:T(8,128)(2,1)} %bitcast.201, f32[2048,1024]{1,0:T(8,128)} %get-tuple-element.132.u_ref, ...), custom_call_target="tpu_custom_call" | custom-call | flops 10737418240 | bytes 29884416 | tf_op jit(solution)/shard_map/outproj_bwd/pallas_call | solution.py:175
  546.6 34.6 %attn_bwd.5 = (f32[2048,256]{1,0:T(8,128)}, f32[2048,256]{1,0:T(8,128)}, f32[2048,256]{1,0:T(8,128)}, f32[2048,256]{1,0:T(8,128)}) custom-call(bf16[2048,256]{1,0:T(8,128)(2,1)} %get-tuple-element.123.refs_1_.k_ref, bf16[2048,256]{1,0:T(8,128)(2,1)} %get-tuple-element.124.refs_3_.v_ref, bf16[2048,256]{1,0:T(8,128)(2,1)} %get-tuple-element.119.q_ref.refs_0_, ...), custom_call_target="tpu_custom_call" | custom-call | flops 21474836480 | bytes 12582912 | tf_op jit(solution)/shard_map/attn_bwd/pallas_call | solution.py:222
  581.2 34.6 %attn_bwd.4 = (f32[2048,256]{1,0:T(8,128)}, f32[2048,256]{1,0:T(8,128)}, f32[2048,256]{1,0:T(8,128)}, f32[2048,256]{1,0:T(8,128)}) custom-call(bf16[2048,256]{1,0:T(8,128)(2,1)} %get-tuple-element.117.refs_0_.k_ref, bf16[2048,256]{1,0:T(8,128)(2,1)} %get-tuple-element.118.refs_2_.v_ref, bf16[2048,256]{1,0:T(8,128)(2,1)} %get-tuple-element.119.q_ref.refs_0_, ...), custom_call_target="tpu_custom_call" | custom-call | flops 21474836480 | bytes 12582912 | tf_op jit(solution)/shard_map/attn_bwd/pallas_call | solution.py:222
  624.3 21.1 %convolution_convert_fusion.3 = bf16[2048,2048]{1,0:T(8,128)(2,1)} fusion(bf16[2048,1792]{1,0:T(8,128)(2,1)} %get-tuple-element.143.refs_2_, bf16[2048,1280]{1,0:T(8,128)(2,1)} %copy-done.5, bf16[2048,256]{1,0:T(8,128)(2,1)S(1)} %copy-done.19, bf16[2048,256]{1,0:T(8,128)(2,1)S(1)} %copy-done.17), kind=kOutput, calls=%fused_computation.9 | convolution fusion | flops 15058599936 | bytes 23068672 | tf_op jit(solution)/shard_map/dot_general | solution.py:520
  674.6 39.7 %wgrad_in.2.refs_5_ = bf16[2,2048,1792]{2,1,0:T(8,128)(2,1)} custom-call(bf16[2048,2048]{1,0:T(8,128)(2,1)} %all-gather.16.cloned.1.call-done.h_ref.refs_0_, bf16[2048,2048]{1,0:T(8,128)(2,1)} %all-gather.18.cloned.1.call-done.h_ref.refs_1_, bf16[2048,1792]{1,0:T(8,128)(2,1)} %get-tuple-element.143.refs_2_, bf16[2048,1792]{1,0:T(8,128)(2,1)} %get-tuple-element.150.refs_3_, ...), custom_call_target="tpu_custom_call" | custom-call | flops 30064771072 | bytes 38797312 | tf_op jit(solution)/shard_map/wgrad_in/pallas_call | solution.py:318
  717.7 26.8 %reduce-scatter.15.cloned.1.call-done = bf16[256,2048]{1,0:T(8,128)(2,1)} async-done(((bf16[2048,2048]{1,0:T(8,128)(2,1)}), bf16[256,2048]{1,0:T(8,128)(2,1)}) %reduce-scatter.15.cloned.1.call-update) | async-done | bytes 1048592 | tf_op jit(solution)/shard_map/reduce_scatter | solution.py:442
  768.1 30.1 %wgrad_out.2.refs_4_ = bf16[2,1280,2048]{2,1,0:T(8,128)(2,1)} custom-call(bf16[2048,1280]{1,0:T(8,128)(2,1)} %get-tuple-element.126.o_ref.refs_0_, bf16[2048,1280]{1,0:T(8,128)(2,1)} %get-tuple-element.128.o_ref.refs_1_, bf16[2048,2048]{1,0:T(8,128)(2,1)} %all-gather.20.cloned.1.call-done.db_ref.refs_2_, ...), custom_call_target="tpu_custom_call" | custom-call | flops 21474836480 | bytes 32505856 | tf_op jit(solution)/shard_map/wgrad_out/pallas_call | solution.py:318
  805.4 22.8 %outproj_bwd.6 = (bf16[2048,256]{1,0:T(8,128)(2,1)}, f32[8,2048]{1,0:T(8,128)}, bf16[2048,1792]{1,0:T(8,128)(2,1)}, f32[1,1024]{1,0:T(1,128)}) custom-call(bf16[2048,2048]{1,0:T(8,128)(2,1)} %all-gather.24.cloned.1.call-done.db_ref.refs_2_, bf16[2048,1280]{1,0:T(8,128)(2,1)} %bitcast.198, f32[2048,1024]{1,0:T(8,128)} %get-tuple-element.159.u_ref, ...), custom_call_target="tpu_custom_call" | custom-call | flops 10737418240 | bytes 29884416 | tf_op jit(solution)/shard_map/outproj_bwd/pallas_call | solution.py:175
  828.2 24.3 %all-gather.26.cloned.1.call-done.db_ref.refs_3_ = bf16[2048,2048]{1,0:T(8,128)(2,1)} async-done(((bf16[256,2048]{1,0:T(8,128)(2,1)}), bf16[2048,2048]{1,0:T(8,128)(2,1)}) %all-gather.26.cloned.1.call-update) | async-done | bytes 8388624 | tf_op jit(solution)/shard_map/all_gather | solution.py:439
  852.6 22.9 %outproj_bwd.7 = (bf16[2048,256]{1,0:T(8,128)(2,1)}, f32[8,2048]{1,0:T(8,128)}, bf16[2048,1792]{1,0:T(8,128)(2,1)}, f32[1,1024]{1,0:T(1,128)}) custom-call(bf16[2048,2048]{1,0:T(8,128)(2,1)} %all-gather.26.cloned.1.call-done.db_ref.refs_3_, bf16[2048,1280]{1,0:T(8,128)(2,1)} %bitcast.199, f32[2048,1024]{1,0:T(8,128)} %get-tuple-element.161.u_ref, ...), custom_call_target="tpu_custom_call" | custom-call | flops 10737418240 | bytes 29884416 | tf_op jit(solution)/shard_map/outproj_bwd/pallas_call | solution.py:175
  875.5 35.1 %attn_bwd.7 = (f32[2048,256]{1,0:T(8,128)}, f32[2048,256]{1,0:T(8,128)}, f32[2048,256]{1,0:T(8,128)}, f32[2048,256]{1,0:T(8,128)}) custom-call(bf16[2048,256]{1,0:T(8,128)(2,1)} %get-tuple-element.106.refs_1_.k_ref, bf16[2048,256]{1,0:T(8,128)(2,1)} %get-tuple-element.108.refs_3_.v_ref, bf16[2048,256]{1,0:T(8,128)(2,1)} %get-tuple-element.104.q_ref.refs_0_, ...), custom_call_target="tpu_custom_call" | custom-call | flops 21474836480 | bytes 12582912 | tf_op jit(solution)/shard_map/attn_bwd/pallas_call | solution.py:222
  910.6 34.7 %attn_bwd.6 = (f32[2048,256]{1,0:T(8,128)}, f32[2048,256]{1,0:T(8,128)}, f32[2048,256]{1,0:T(8,128)}, f32[2048,256]{1,0:T(8,128)}) custom-call(bf16[2048,256]{1,0:T(8,128)(2,1)} %get-tuple-element.105.refs_0_.k_ref, bf16[2048,256]{1,0:T(8,128)(2,1)} %get-tuple-element.107.refs_2_.v_ref, bf16[2048,256]{1,0:T(8,128)(2,1)} %get-tuple-element.104.q_ref.refs_0_, ...), custom_call_target="tpu_custom_call" | custom-call | flops 21474836480 | bytes 12582912 | tf_op jit(solution)/shard_map/attn_bwd/pallas_call | solution.py:222
  953.6 20.7 %convolution_convert_fusion.1 = bf16[2048,2048]{1,0:T(8,128)(2,1)} fusion(bf16[2048,1792]{1,0:T(8,128)(2,1)} %get-tuple-element.172.refs_2_, bf16[2048,1280]{1,0:T(8,128)(2,1)} %copy-done.4, bf16[2048,256]{1,0:T(8,128)(2,1)S(1)} %copy-done.22, bf16[2048,256]{1,0:T(8,128)(2,1)S(1)} %copy-done.24), kind=kOutput, calls=%fused_computation.7 | convolution fusion | flops 15058599936 | bytes 23068672 | tf_op jit(solution)/shard_map/dot_general | solution.py:520
  1039.6 30.1 %wgrad_out.3 = bf16[2,1280,2048]{2,1,0:T(8,128)(2,1)} custom-call(bf16[2048,1280]{1,0:T(8,128)(2,1)} %get-tuple-element.110.o_ref.refs_0_, bf16[2048,1280]{1,0:T(8,128)(2,1)} %get-tuple-element.113.o_ref.refs_1_, bf16[2048,2048]{1,0:T(8,128)(2,1)} %all-gather.24.cloned.1.call-done.db_ref.refs_2_, ...), custom_call_target="tpu_custom_call", output_to_operand_aliasing={{}: (4, {})} | custom-call | flops 21474836480 | bytes 32505856 | tf_op jit(solution)/shard_map/wgrad_out/pallas_call | solution.py:318
  1069.8 39.8 %wgrad_in.3 = bf16[2,2048,1792]{2,1,0:T(8,128)(2,1)} custom-call(bf16[2048,2048]{1,0:T(8,128)(2,1)} %all-gather.10.cloned.1.call-done.h_ref.refs_0_, bf16[2048,2048]{1,0:T(8,128)(2,1)} %all-gather.14.cloned.1.call-done.h_ref.refs_1_, bf16[2048,1792]{1,0:T(8,128)(2,1)} %get-tuple-element.172.refs_2_, ...), custom_call_target="tpu_custom_call", output_to_operand_aliasing={{}: (5, {})} | custom-call | flops 30064771072 | bytes 38797312 | tf_op jit(solution)/shard_map/wgrad_in/pallas_call | solution.py:318
  (371 shorter events, 434.2 us)
Async XLA Ops:
  7.2 36.8 %all-gather.12.cloned.1.call-start = ((), (), s32[]{:S(2)}) async-start(), calls=%async_computation.9 | async-start | bytes 4718592 | tf_op jit(solution)/shard_map/all_gather | solution.py:449
  9.2 79.6 %all-gather.14.cloned.1.call-start = ((), (), s32[]{:S(2)}) async-start(), calls=%async_computation.10 | async-start | bytes 9437184 | tf_op jit(solution)/shard_map/all_gather | solution.py:439
  23.2 270.6 %copy-start.30 = (f32[1,2048]{1,0:T(1,128)}, f32[1,2048]{1,0:T(1,128)S(1)}, u32[]{:S(2)}) copy-start(f32[1,2048]{1,0:T(1,128)S(1)} %get-tuple-element.264) | copy-start | bytes 24580
  25.6 111.1 %all-gather.10.cloned.1.call-start = ((), (), s32[]{:S(2)}) async-start(), calls=%async_computation.8 | async-start | bytes 9437184 | tf_op jit(solution)/shard_map/all_gather | solution.py:439
  26.4 214.2 %reduce-scatter.9.cloned.1.call-start = ((), (), s32[]{:S(2)}) async-start(), calls=%async_computation.11 | async-start | bytes 9437184 | tf_op jit(solution)/shard_map/reduce_scatter | solution.py:442
  192.7 98.8 %reduce-scatter.11.cloned.1.call-start = ((), (), s32[]{:S(2)}) async-start(), calls=%async_computation.12 | async-start | bytes 9437184 | tf_op jit(solution)/shard_map/reduce_scatter | solution.py:442
  225.1 120.7 %all-gather.18.cloned.1.call-start = ((), (), s32[]{:S(2)}) async-start(), calls=%async_computation.14 | async-start | bytes 9437184 | tf_op jit(solution)/shard_map/all_gather | solution.py:439
  225.8 132.0 %copy-start.20 = (bf16[256,256]{1,0:T(8,128)(2,1)}, bf16[256,256]{1,0:T(8,128)(2,1)S(1)}, u32[]{:S(2)}) copy-start(bf16[256,256]{1,0:T(8,128)(2,1)S(1)} %fusion.71.refs_4_) | copy-start | bytes 393220
  226.4 67.4 %copy-start.35 = (f32[1,2048]{1,0:T(1,128)}, f32[1,2048]{1,0:T(1,128)S(1)}, u32[]{:S(2)}) copy-start(f32[1,2048]{1,0:T(1,128)S(1)} %get-tuple-element.268) | copy-start | bytes 24580
  236.6 60.8 %copy-start.25 = (f32[1,2048]{1,0:T(1,128)}, f32[1,2048]{1,0:T(1,128)S(1)}, u32[]{:S(2)}) copy-start(f32[1,2048]{1,0:T(1,128)S(1)} %get-tuple-element.261) | copy-start | bytes 24580
  236.6 64.0 %copy-start.42 = (f32[1,2048]{1,0:T(1,128)}, f32[1,2048]{1,0:T(1,128)S(1)}, u32[]{:S(2)}) copy-start(f32[1,2048]{1,0:T(1,128)S(1)} %get-tuple-element.259) | copy-start | bytes 24580
  299.7 93.9 %all-gather.16.cloned.1.call-start = ((), (), s32[]{:S(2)}) async-start(), calls=%async_computation.13 | async-start | bytes 9437184 | tf_op jit(solution)/shard_map/all_gather | solution.py:439
  300.5 181.3 %all-gather.20.cloned.1.call-start = ((), (), s32[]{:S(2)}) async-start(), calls=%async_computation.15 | async-start | bytes 9437184 | tf_op jit(solution)/shard_map/all_gather | solution.py:439
  349.0 174.8 %all-gather.22.cloned.1.call-start = ((), (), s32[]{:S(2)}) async-start(), calls=%async_computation.16 | async-start | bytes 9437184 | tf_op jit(solution)/shard_map/all_gather | solution.py:439
  349.8 364.6 %reduce-scatter.17.cloned.1.call-start = ((), (), s32[]{:S(2)}) async-start(), calls=%async_computation.19 | async-start | bytes 9437184 | tf_op jit(solution)/shard_map/reduce_scatter | solution.py:442
  481.9 232.5 %reduce-scatter.19.cloned.1.call-start = ((), (), s32[]{:S(2)}) async-start(), calls=%async_computation.20 | async-start | bytes 9437184 | tf_op jit(solution)/shard_map/reduce_scatter | solution.py:442
  482.7 235.0 %reduce-scatter.13.cloned.1.call-start = ((), (), s32[]{:S(2)}) async-start(), calls=%async_computation.17 | async-start | bytes 9437184 | tf_op jit(solution)/shard_map/reduce_scatter | solution.py:442
  645.5 98.9 %reduce-scatter.15.cloned.1.call-start = ((), (), s32[]{:S(2)}) async-start(), calls=%async_computation.18 | async-start | bytes 9437184 | tf_op jit(solution)/shard_map/reduce_scatter | solution.py:442
  674.5 130.9 %all-gather.24.cloned.1.call-start = ((), (), s32[]{:S(2)}) async-start(), calls=%async_computation.21 | async-start | bytes 9437184 | tf_op jit(solution)/shard_map/all_gather | solution.py:439
  759.3 93.2 %all-gather.26.cloned.1.call-start = ((), (), s32[]{:S(2)}) async-start(), calls=%async_computation.22 | async-start | bytes 9437184 | tf_op jit(solution)/shard_map/all_gather | solution.py:439
  760.0 349.7 %reduce-scatter.21.cloned.1.call-start = ((), (), s32[]{:S(2)}) async-start(), calls=%async_computation.23 | async-start | bytes 9437184 | tf_op jit(solution)/shard_map/reduce_scatter | solution.py:442
  974.4 135.2 %reduce-scatter.23.cloned.1.call-start = ((), (), s32[]{:S(2)}) async-start(), calls=%async_computation.24 | async-start | bytes 9437184 | tf_op jit(solution)/shard_map/reduce_scatter | solution.py:442
  1069.8 39.9 %copy-start.41 = (f32[512]{0:T(512)S(1)}, f32[512]{0:T(512)}, u32[]{:S(2)}) copy-start(f32[512]{0:T(512)} %copy-done.40) | copy-start | bytes 6148
  1069.8 42.6 %copy-start.60 = (f32[512]{0:T(512)S(1)}, f32[512]{0:T(512)}, u32[]{:S(2)}) copy-start(f32[512]{0:T(512)} %copy-done.59) | copy-start | bytes 6148
  (74 other events, 783.8 us)
Sparse Core Ops, SparseCore 0:
  10.2 31.1 all-gather.11
  43.5 45.2 all-gather.13
  91.0 45.6 all-gather.9
  192.8 47.7 reduce-scatter.8
  243.4 48.1 reduce-scatter.10
  299.8 45.9 all-gather.17
  348.0 45.6 all-gather.15
  395.3 45.6 all-gather.19
  442.6 45.6 all-gather.21
  490.4 47.7 reduce-scatter.16
  540.5 48.0 reduce-scatter.18
  645.6 47.7 reduce-scatter.12
  696.3 48.0 reduce-scatter.14
  759.5 45.9 all-gather.23
  806.9 45.6 all-gather.25
  974.6 50.9 reduce-scatter.20
  1027.7 48.0 reduce-scatter.22

commit v2 on v1

--- a/solution.py
+++ b/solution.py
@@ -46,31 +46,43 @@
     h = h_ref[...]
     cos = cs_ref[:, :half]
     sin = cs_ref[:, half:]
-    for part, (s_ref, o_ref, post) in enumerate(((qs_ref, q_ref, hd ** -0.5), (ks_ref, k_ref, None))):
-        lo = part * hd
-        y = dot(h, w_ref[:, lo:lo + hd]) + b_ref[:, lo:lo + hd]
+    mlp = u_ref.shape[1]
+
+    def proj(lo, width):
+        return dot(h, w_ref[:, lo:lo + width]) + b_ref[:, lo:lo + width]
+
+    def finish_qk(y, lo, s_ref, o_ref, post):
         yqk_ref[:, lo:lo + hd] = y
         inv = lax.rsqrt(jnp.mean(y * y, axis=-1, keepdims=True) + NORM_EPS)
         t = y * inv * s_ref[...]
         ta, tb = t[:, :half], t[:, half:]
-        ra = ta * cos - tb * sin
-        rb = ta * sin + tb * cos
-        ra = ra.astype(BF16)
-        rb = rb.astype(BF16)
+        ra = (ta * cos - tb * sin).astype(BF16)
+        rb = (ta * sin + tb * cos).astype(BF16)
         if post is not None:
             ra = ra * BF16(post)
             rb = rb * BF16(post)
         o_ref[:, :half] = ra
         o_ref[:, half:] = rb
-    v_ref[...] = (dot(h, w_ref[:, 2 * hd:3 * hd]) + b_ref[:, 2 * hd:3 * hd]).astype(BF16)
-    j_ref[:, :hd] = jnp.zeros((h.shape[0], hd), BF16)
-    mlp = u_ref.shape[1]
-    for lo in range(0, mlp, 256):
-        c0 = 3 * hd + lo
-        u = dot(h, w_ref[:, c0:c0 + 256]) + b_ref[:, c0:c0 + 256]
+
+    def finish_mlp(u, lo):
         u_ref[:, lo:lo + 256] = u
         g = 0.5 * u * (1.0 + jnp.tanh(GELU_A * (u + GELU_B * (u * u * u))))
         j_ref[:, hd + lo:hd + lo + 256] = g.astype(BF16)
+
+    def finish_v(v):
+        v_ref[...] = v.astype(BF16)
+        j_ref[:, :hd] = jnp.zeros((h.shape[0], hd), BF16)
+
+    steps = [(0, hd, lambda y: finish_qk(y, 0, qs_ref, q_ref, hd ** -0.5)),
+             (hd, hd, lambda y: finish_qk(y, hd, ks_ref, k_ref, None))]
+    steps += [(3 * hd + lo, 256, lambda u, lo=lo: finish_mlp(u, lo)) for lo in range(0, mlp, 256)]
+    steps += [(2 * hd, hd, finish_v)]
+    ahead = proj(*steps[0][:2])
+    for idx, step in enumerate(steps):
+        now = ahead
+        if idx + 1 < len(steps):
+            ahead = proj(*steps[idx + 1][:2])
+        step[2](now)
 
 
 def inproj(h, w, b, qs, ks, cs):
@@ -146,24 +158,28 @@
     hd = do_ref.shape[1]
     mlp = u_ref.shape[1]
     db = db_ref[...]
-    do = dot(db, w_ref[:, :hd]).astype(BF16)
-    do_ref[...] = do
-    delta_ref[...] = as_row(jnp.sum(do.astype(F32) * o_ref[...].astype(F32), axis=-1, keepdims=True))
 
     @pl.when(pl.program_id(0) == 0)
     def _():
         gb_ref[...] = jnp.zeros_like(gb_ref)
 
+    def part(lo):
+        return dot(db, w_ref[:, hd + lo:hd + lo + 256])
+
+    ahead = part(0)
     for lo in range(0, mlp, 256):
-        dm = dot(db, w_ref[:, hd + lo:hd + lo + 256]).astype(BF16).astype(F32)
+        dm = ahead.astype(BF16).astype(F32)
+        ahead = part(lo + 256) if lo + 256 < mlp else dot(db, w_ref[:, :hd])
         u = u_ref[:, lo:lo + 256]
         u2 = u * u
-        t = jnp.tanh(GELU_A * (u + GELU_B * (u2 * u)))
-        grad = 0.5 * (1.0 + t) + 0.5 * u * (1.0 - t * t) * (GELU_A * (1.0 + 3.0 * GELU_B * u2))
+        t = jnp.tanh(u * (GELU_A + (GELU_A * GELU_B) * u2))
+        grad = 0.5 + 0.5 * t + (u * (1.0 - t * t)) * (0.5 * GELU_A + (1.5 * GELU_A * GELU_B) * u2)
         du = dm * grad
         gb_ref[:, lo:lo + 256] += jnp.sum(du, axis=0, keepdims=True)
         dp_ref[:, 3 * hd + lo:3 * hd + lo + 256] = du.astype(BF16)
-    dp_ref[:, :3 * hd] = jnp.zeros((db.shape[0], 3 * hd), BF16)
+    do = ahead.astype(BF16)
+    do_ref[...] = do
+    delta_ref[...] = as_row(jnp.sum(do.astype(F32) * o_ref[...].astype(F32), axis=-1, keepdims=True))
 
 
 def outproj_bwd(db, wt, u, joined):
@@ -197,21 +213,29 @@
         for c in range(nc):
             dq_refs[c][...] = jnp.zeros_like(dq_refs[c])
 
-    dk_ref[...] = jnp.zeros_like(dk_ref)
-    dv_ref[...] = jnp.zeros_like(dv_ref)
-    for c in range(nc):
-        @pl.loop(0, q_refs[c].shape[0] // bq)
-        def _(t, c=c):
-            at = pl.ds(pl.multiple_of(t * bq, bq), bq)
-            q = q_refs[c][at, :]
-            do = do_refs[c][at, :]
-            s = dot(k, q, ((1,), (1,)))
-            dp = dot(v, do, ((1,), (1,)))
-            p = jnp.exp(s - lse_refs[c][:1, at])
-            dv_ref[...] += dot(p.astype(BF16), do)
-            ds = (p * (dp - dl_refs[c][:1, at])).astype(BF16)
-            dk_ref[...] += dot(ds, q)
-            dq_refs[c][at, :] += dot(ds, k, ((0,), (0,)))
+    pieces = [(c, t) for c in range(nc) for t in range(0, q_refs[0].shape[0], bq)]
+
+    def start(idx):
+        c, t = pieces[idx]
+        q = q_refs[c][t:t + bq, :]
+        do = do_refs[c][t:t + bq, :]
+        return q, do, dot(k, q, ((1,), (1,))), dot(v, do, ((1,), (1,)))
+
+    dk_sum = dv_sum = None
+    ahead = start(0)
+    for idx, (c, t) in enumerate(pieces):
+        q, do, s, dp = ahead
+        if idx + 1 < len(pieces):
+            ahead = start(idx + 1)
+        p = jnp.exp(s - lse_refs[c][:1, t:t + bq])
+        ds = (p * (dp - dl_refs[c][:1, t:t + bq])).astype(BF16)
+        dv_part = dot(p.astype(BF16), do)
+        dk_part = dot(ds, q)
+        dv_sum = dv_part if dv_sum is None else dv_sum + dv_part
+        dk_sum = dk_part if dk_sum is None else dk_sum + dk_part
+        dq_refs[c][t:t + bq, :] += dot(ds, k, ((0,), (0,)))
+    dk_ref[...] = dk_sum
+    dv_ref[...] = dv_sum
 
 
 def attention_bwd(k, v, qs, dos, lses, deltas, bq=512, bk=512):
@@ -484,7 +508,11 @@
                 zs.append(jnp.dot(js[c], w_o[l], preferred_element_type=F32).astype(BF16))
             if l == nb - 1:
                 db_last[0], zs = lax.optimization_barrier((db_last[0], zs))
-            mixed = jnp.concatenate(scatter(zs), axis=0)
+            mixed = scatter(zs)
+            if l == 0 and nb > 1:
+                prep = (w_perm[1], b_perm[1], mods[1], list(w_ot))
+                mixed, (w_perm[1], b_perm[1], mods[1], w_ot[:]) = lax.optimization_barrier((mixed, prep))
+            mixed = jnp.concatenate(mixed, axis=0)
             if l < nb - 1:
                 branch = mixed.astype(F32) + b_out[l].astype(F32)
                 x_cur = (x_f32 + gate * branch).astype(BF16)
@@ -501,7 +529,7 @@
             d_bout = jnp.sum(gated, axis=0)
             db = db_last if l == nb - 1 else gather(gated.astype(BF16))
             if l < nb - 1:
-                db[0], g_win, g_wout = lax.optimization_barrier((db[0], g_win, g_wout))
+                db[0], g_win, g_wout, g_wmod = lax.optimization_barrier((db[0], g_win, g_wout, g_wmod))
             back = [outproj_bwd(db[c], w_ot[l], us[c], js[c]) for c in range(nc)]
             dos, deltas, dprojs, gbu = map(list, zip(*back))
             dqs = [[] for _ in range(nc)]

time: 1170 us -> 1090 us (0.932)
  waiting for transfers between devices: 229 us -> 184 us
  Pallas kernels: 615 us -> 584 us
    reduce_scatter x8, waiting for transfers between devices: 79.4 us -> 44.7 us  [scatter(): lax.psum_scatter(p, 'tp', scatter_dimension=0, tiled=True)]
    pallas_call x4, Pallas kernels: 139 us -> 112 us  [attention_bwd(): call(functools.partial(attn_bwd_body, nc, bq), grid=(s // bk,), in_specs=...]
  transfers between devices with their start and end apart: 17 -> 17, of which waited for: 9 -> 7; matrix products, arithmetic and copies ran while one was open for 19% -> 20% of each run, Pallas kernels for 39% -> 40%
where the time goes in v2:
time: 1090 us; the launch traced here: 1080 us
  Pallas kernels  584 us (54%)
  waiting for transfers between devices  184 us (17%)
  matrix products  175 us (16%)
  local copies, waits for them, and re-layouts  67.8 us (6%)
  other arithmetic  55.2 us (5%)
  between operations  15.5 us (1%)
    pallas_call x4, Pallas kernels, wgrad(): call(functools.partial(wgrad_body, nc, sel is not None), grid=(m // tile,...  140 us
    all_gather x8, waiting for transfers between devices, gather(): lax.all_gather(t[c * cw:(c + 1) * cw], 'tp', axis=0, tiled=True)  135 us
    pallas_call x4, Pallas kernels, attention_bwd(): call(functools.partial(attn_bwd_body, nc, bq), grid=(s // bk,), in_specs=...  112 us
    pallas_call x4, Pallas kernels, inproj(): call(inproj_body, grid=(s // tile,), in_specs=[rows(tile, d), full((d, n)...  94.6 us
    pallas_call x4, Pallas kernels, outproj_bwd(): call(outproj_bwd_body, grid=(s // tile,), in_specs=[rows(tile, d), full((...  84.3 us
    dot_general x4, matrix products, device_fn(): lax.dot_general(dprojs[c], w_perm[l], (((1,), (1,)), ((), ())), preferred...  84.1 us
    dot_general x4, matrix products, device_fn(): zs.append(jnp.dot(js[c], w_o[l], preferred_element_type=F32).astype(BF16))  66.3 us
    pallas_call x4, Pallas kernels, attention(): call(functools.partial(attn_body, nc, bk), grid=(s // bq,), in_specs=[row...  63.1 us
  transfers between devices with their start and end apart: 17, of which 7 were waited for; matrix products, arithmetic and copies ran while one was open for 20% of the time, Pallas kernels for 40%

profile of v2, /device:TPU:113, one launch (start us, length us, event | category | flops | bytes accessed | tf_op | source)
XLA Modules:
  0.0 1082.5 jit_solution(2899020814985080072)
XLA Ops:
  50.4 38.4 %all-gather.14.cloned.1.call-done.h_ref.refs_1_ = bf16[2048,2048]{1,0:T(8,128)(2,1)} async-done(((bf16[256,2048]{1,0:T(8,128)(2,1)}), bf16[2048,2048]{1,0:T(8,128)(2,1)}) %all-gather.14.cloned.1.call-update) | async-done | bytes 8388624 | tf_op jit(solution)/shard_map/all_gather | solution.py:463
  88.8 23.7 %inproj.5 = (bf16[2048,256]{1,0:T(8,128)(2,1)}, bf16[2048,256]{1,0:T(8,128)(2,1)}, bf16[2048,256]{1,0:T(8,128)(2,1)}, bf16[2048,1280]{1,0:T(8,128)(2,1)}, f32[2048,512]{1,0:T(8,128)}, /*index=5*/f32[2048,1024]{1,0:T(8,128)}) custom-call(bf16[2048,2048]{1,0:T(8,128)(2,1)} %all-gather.14.cloned.1.call-done.h_ref.refs_1_, ...), custom_call_target="tpu_custom_call" | custom-call | flops 15032385536 | bytes 37748736 | tf_op jit(solution)/shard_map/inproj/pallas_call | solution.py:94
  112.5 24.1 %all-gather.10.cloned.1.call-done.h_ref.refs_0_ = bf16[2048,2048]{1,0:T(8,128)(2,1)} async-done(((bf16[256,2048]{1,0:T(8,128)(2,1)}), bf16[2048,2048]{1,0:T(8,128)(2,1)}) %all-gather.10.cloned.1.call-update) | async-done | bytes 8388624 | tf_op jit(solution)/shard_map/all_gather | solution.py:463
  136.7 23.5 %inproj.4 = (bf16[2048,256]{1,0:T(8,128)(2,1)}, bf16[2048,256]{1,0:T(8,128)(2,1)}, bf16[2048,256]{1,0:T(8,128)(2,1)}, bf16[2048,1280]{1,0:T(8,128)(2,1)}, f32[2048,512]{1,0:T(8,128)}, /*index=5*/f32[2048,1024]{1,0:T(8,128)}) custom-call(bf16[2048,2048]{1,0:T(8,128)(2,1)} %all-gather.10.cloned.1.call-done.h_ref.refs_0_, ...), custom_call_target="tpu_custom_call" | custom-call | flops 15032385536 | bytes 37748736 | tf_op jit(solution)/shard_map/inproj/pallas_call | solution.py:94
  301.0 43.4 %all-gather.18.cloned.1.call-done.h_ref.refs_1_ = bf16[2048,2048]{1,0:T(8,128)(2,1)} async-done(((bf16[256,2048]{1,0:T(8,128)(2,1)}), bf16[2048,2048]{1,0:T(8,128)(2,1)}) %all-gather.18.cloned.1.call-update) | async-done | bytes 8388624 | tf_op jit(solution)/shard_map/all_gather | solution.py:463
  350.0 23.8 %inproj.7 = (bf16[2048,256]{1,0:T(8,128)(2,1)}, bf16[2048,256]{1,0:T(8,128)(2,1)}, bf16[2048,256]{1,0:T(8,128)(2,1)}, bf16[2048,1280]{1,0:T(8,128)(2,1)}, f32[2048,512]{1,0:T(8,128)}, /*index=5*/f32[2048,1024]{1,0:T(8,128)}) custom-call(bf16[2048,2048]{1,0:T(8,128)(2,1)} %all-gather.18.cloned.1.call-done.h_ref.refs_1_, ...), custom_call_target="tpu_custom_call" | custom-call | flops 15032385536 | bytes 37748736 | tf_op jit(solution)/shard_map/inproj/pallas_call | solution.py:94
  392.3 23.6 %inproj.6 = (bf16[2048,256]{1,0:T(8,128)(2,1)}, bf16[2048,256]{1,0:T(8,128)(2,1)}, bf16[2048,256]{1,0:T(8,128)(2,1)}, bf16[2048,1280]{1,0:T(8,128)(2,1)}, f32[2048,512]{1,0:T(8,128)}, /*index=5*/f32[2048,1024]{1,0:T(8,128)}) custom-call(bf16[2048,2048]{1,0:T(8,128)(2,1)} %all-gather.16.cloned.1.call-done.h_ref.refs_0_, ...), custom_call_target="tpu_custom_call" | custom-call | flops 15032385536 | bytes 37748736 | tf_op jit(solution)/shard_map/inproj/pallas_call | solution.py:94
  481.4 21.2 %outproj_bwd.4 = (bf16[2048,256]{1,0:T(8,128)(2,1)}, f32[8,2048]{1,0:T(8,128)}, bf16[2048,1792]{1,0:T(8,128)(2,1)}, f32[1,1024]{1,0:T(1,128)}) custom-call(bf16[2048,2048]{1,0:T(8,128)(2,1)} %all-gather.20.cloned.1.call-done.db_ref.refs_2_, bf16[2048,1280]{1,0:T(8,128)(2,1)} %bitcast.202, f32[2048,1024]{1,0:T(8,128)} %get-tuple-element.148.u_ref, ...), custom_call_target="tpu_custom_call" | custom-call | flops 10737418240 | bytes 29884416 | tf_op jit(solution)/shard_map/outproj_bwd/pallas_call | solution.py:191
  502.6 21.0 %outproj_bwd.5 = (bf16[2048,256]{1,0:T(8,128)(2,1)}, f32[8,2048]{1,0:T(8,128)}, bf16[2048,1792]{1,0:T(8,128)(2,1)}, f32[1,1024]{1,0:T(1,128)}) custom-call(bf16[2048,2048]{1,0:T(8,128)(2,1)} %all-gather.22.cloned.1.call-done.db_ref.refs_3_, bf16[2048,1280]{1,0:T(8,128)(2,1)} %bitcast.203, f32[2048,1024]{1,0:T(8,128)} %get-tuple-element.150.u_ref, ...), custom_call_target="tpu_custom_call" | custom-call | flops 10737418240 | bytes 29884416 | tf_op jit(solution)/shard_map/outproj_bwd/pallas_call | solution.py:191
  523.6 27.8 %attn_bwd.5 = (f32[2048,256]{1,0:T(8,128)}, f32[2048,256]{1,0:T(8,128)}, f32[2048,256]{1,0:T(8,128)}, f32[2048,256]{1,0:T(8,128)}) custom-call(bf16[2048,256]{1,0:T(8,128)(2,1)} %get-tuple-element.140.refs_1_.k_ref, bf16[2048,256]{1,0:T(8,128)(2,1)} %get-tuple-element.141.refs_3_.v_ref, bf16[2048,256]{1,0:T(8,128)(2,1)} %get-tuple-element.136.q_ref.refs_0_, ...), custom_call_target="tpu_custom_call" | custom-call | flops 21474836480 | bytes 12582912 | tf_op jit(solution)/shard_map/attn_bwd/pallas_call | solution.py:246
  551.5 28.0 %attn_bwd.4 = (f32[2048,256]{1,0:T(8,128)}, f32[2048,256]{1,0:T(8,128)}, f32[2048,256]{1,0:T(8,128)}, f32[2048,256]{1,0:T(8,128)}) custom-call(bf16[2048,256]{1,0:T(8,128)(2,1)} %get-tuple-element.134.refs_0_.k_ref, bf16[2048,256]{1,0:T(8,128)(2,1)} %get-tuple-element.135.refs_2_.v_ref, bf16[2048,256]{1,0:T(8,128)(2,1)} %get-tuple-element.136.q_ref.refs_0_, ...), custom_call_target="tpu_custom_call" | custom-call | flops 21474836480 | bytes 12582912 | tf_op jit(solution)/shard_map/attn_bwd/pallas_call | solution.py:246
  587.7 21.3 %convolution_convert_fusion.3 = bf16[2048,2048]{1,0:T(8,128)(2,1)} fusion(bf16[2048,1792]{1,0:T(8,128)(2,1)} %get-tuple-element.161.refs_2_, bf16[2048,1792]{1,0:T(8,128)(2,1)} %pad_maximum_fusion.1.w_ref), kind=kOutput, calls=%fused_computation.9 | convolution fusion | flops 15036579840 | bytes 23068672 | tf_op jit(solution)/shard_map/dot_general | solution.py:548
  617.7 21.3 %convolution_convert_fusion.2 = bf16[2048,2048]{1,0:T(8,128)(2,1)} fusion(bf16[2048,1792]{1,0:T(8,128)(2,1)} %get-tuple-element.168.refs_3_, bf16[2048,1792]{1,0:T(8,128)(2,1)} %pad_maximum_fusion.1.w_ref), kind=kOutput, calls=%fused_computation.8 | convolution fusion | flops 15036579840 | bytes 23068672 | tf_op jit(solution)/shard_map/dot_general | solution.py:548
  639.1 39.5 %wgrad_in.2.refs_5_ = bf16[2,2048,1792]{2,1,0:T(8,128)(2,1)} custom-call(bf16[2048,2048]{1,0:T(8,128)(2,1)} %all-gather.16.cloned.1.call-done.h_ref.refs_0_, bf16[2048,2048]{1,0:T(8,128)(2,1)} %all-gather.18.cloned.1.call-done.h_ref.refs_1_, bf16[2048,1792]{1,0:T(8,128)(2,1)} %get-tuple-element.161.refs_2_, bf16[2048,1792]{1,0:T(8,128)(2,1)} %get-tuple-element.168.refs_3_, ...), custom_call_target="tpu_custom_call" | custom-call | flops 30064771072 | bytes 38797312 | tf_op jit(solution)/shard_map/wgrad_in/pallas_call | solution.py:342
  682.0 26.0 %reduce-scatter.15.cloned.1.call-done = bf16[256,2048]{1,0:T(8,128)(2,1)} async-done(((bf16[2048,2048]{1,0:T(8,128)(2,1)}), bf16[256,2048]{1,0:T(8,128)(2,1)}) %reduce-scatter.15.cloned.1.call-update) | async-done | bytes 1048592 | tf_op jit(solution)/shard_map/reduce_scatter | solution.py:466
  723.8 30.3 %wgrad_out.2.refs_4_ = bf16[2,1280,2048]{2,1,0:T(8,128)(2,1)} custom-call(bf16[2048,1280]{1,0:T(8,128)(2,1)} %get-tuple-element.143.o_ref.refs_0_, bf16[2048,1280]{1,0:T(8,128)(2,1)} %get-tuple-element.145.o_ref.refs_1_, bf16[2048,2048]{1,0:T(8,128)(2,1)} %all-gather.20.cloned.1.call-done.db_ref.refs_2_, ...), custom_call_target="tpu_custom_call" | custom-call | flops 21474836480 | bytes 32505856 | tf_op jit(solution)/shard_map/wgrad_out/pallas_call | solution.py:342
  786.8 21.0 %outproj_bwd.6 = (bf16[2048,256]{1,0:T(8,128)(2,1)}, f32[8,2048]{1,0:T(8,128)}, bf16[2048,1792]{1,0:T(8,128)(2,1)}, f32[1,1024]{1,0:T(1,128)}) custom-call(bf16[2048,2048]{1,0:T(8,128)(2,1)} %all-gather.24.cloned.1.call-done.db_ref.refs_2_, bf16[2048,1280]{1,0:T(8,128)(2,1)} %bitcast.200, f32[2048,1024]{1,0:T(8,128)} %get-tuple-element.180.u_ref, ...), custom_call_target="tpu_custom_call" | custom-call | flops 10737418240 | bytes 29884416 | tf_op jit(solution)/shard_map/outproj_bwd/pallas_call | solution.py:191
  818.1 21.1 %outproj_bwd.7 = (bf16[2048,256]{1,0:T(8,128)(2,1)}, f32[8,2048]{1,0:T(8,128)}, bf16[2048,1792]{1,0:T(8,128)(2,1)}, f32[1,1024]{1,0:T(1,128)}) custom-call(bf16[2048,2048]{1,0:T(8,128)(2,1)} %all-gather.26.cloned.1.call-done.db_ref.refs_3_, bf16[2048,1280]{1,0:T(8,128)(2,1)} %bitcast.201, f32[2048,1024]{1,0:T(8,128)} %get-tuple-element.182.u_ref, ...), custom_call_target="tpu_custom_call" | custom-call | flops 10737418240 | bytes 29884416 | tf_op jit(solution)/shard_map/outproj_bwd/pallas_call | solution.py:191
  839.2 28.2 %attn_bwd.7 = (f32[2048,256]{1,0:T(8,128)}, f32[2048,256]{1,0:T(8,128)}, f32[2048,256]{1,0:T(8,128)}, f32[2048,256]{1,0:T(8,128)}) custom-call(bf16[2048,256]{1,0:T(8,128)(2,1)} %get-tuple-element.116.refs_1_.k_ref, bf16[2048,256]{1,0:T(8,128)(2,1)} %get-tuple-element.118.refs_3_.v_ref, bf16[2048,256]{1,0:T(8,128)(2,1)} %get-tuple-element.114.q_ref.refs_0_, ...), custom_call_target="tpu_custom_call" | custom-call | flops 21474836480 | bytes 12582912 | tf_op jit(solution)/shard_map/attn_bwd/pallas_call | solution.py:246
  867.3 27.8 %attn_bwd.6 = (f32[2048,256]{1,0:T(8,128)}, f32[2048,256]{1,0:T(8,128)}, f32[2048,256]{1,0:T(8,128)}, f32[2048,256]{1,0:T(8,128)}) custom-call(bf16[2048,256]{1,0:T(8,128)(2,1)} %get-tuple-element.115.refs_0_.k_ref, bf16[2048,256]{1,0:T(8,128)(2,1)} %get-tuple-element.117.refs_2_.v_ref, bf16[2048,256]{1,0:T(8,128)(2,1)} %get-tuple-element.114.q_ref.refs_0_, ...), custom_call_target="tpu_custom_call" | custom-call | flops 21474836480 | bytes 12582912 | tf_op jit(solution)/shard_map/attn_bwd/pallas_call | solution.py:246
  903.5 20.9 %convolution_convert_fusion.1 = bf16[2048,2048]{1,0:T(8,128)(2,1)} fusion(bf16[2048,1792]{1,0:T(8,128)(2,1)} %get-tuple-element.193.refs_2_, bf16[2048,1280]{1,0:T(8,128)(2,1)} %copy-done.5, bf16[2048,256]{1,0:T(8,128)(2,1)S(1)} %copy-done.19, bf16[2048,256]{1,0:T(8,128)(2,1)S(1)} %copy-done.21), kind=kOutput, calls=%fused_computation.7 | convolution fusion | flops 15058599936 | bytes 23068672 | tf_op jit(solution)/shard_map/dot_general | solution.py:548
  932.7 20.7 %convolution_convert_fusion = bf16[2048,2048]{1,0:T(8,128)(2,1)} fusion(bf16[2048,1792]{1,0:T(8,128)(2,1)} %get-tuple-element.200.refs_3_, bf16[2048,1280]{1,0:T(8,128)(2,1)} %copy-done.5, bf16[2048,256]{1,0:T(8,128)(2,1)S(1)} %copy-done.19, bf16[2048,256]{1,0:T(8,128)(2,1)S(1)} %copy-done.21), kind=kOutput, calls=%fused_computation.6 | convolution fusion | flops 15058599936 | bytes 23068672 | tf_op jit(solution)/shard_map/dot_general | solution.py:548
  957.8 30.1 %wgrad_out.3 = bf16[2,1280,2048]{2,1,0:T(8,128)(2,1)} custom-call(bf16[2048,1280]{1,0:T(8,128)(2,1)} %get-tuple-element.120.o_ref.refs_0_, bf16[2048,1280]{1,0:T(8,128)(2,1)} %get-tuple-element.123.o_ref.refs_1_, bf16[2048,2048]{1,0:T(8,128)(2,1)} %all-gather.24.cloned.1.call-done.db_ref.refs_2_, ...), custom_call_target="tpu_custom_call", output_to_operand_aliasing={{}: (4, {})} | custom-call | flops 21474836480 | bytes 32505856 | tf_op jit(solution)/shard_map/wgrad_out/pallas_call | solution.py:342
  988.0 39.8 %wgrad_in.3 = bf16[2,2048,1792]{2,1,0:T(8,128)(2,1)} custom-call(bf16[2048,2048]{1,0:T(8,128)(2,1)} %all-gather.10.cloned.1.call-done.h_ref.refs_0_, bf16[2048,2048]{1,0:T(8,128)(2,1)} %all-gather.14.cloned.1.call-done.h_ref.refs_1_, bf16[2048,1792]{1,0:T(8,128)(2,1)} %get-tuple-element.193.refs_2_, ...), custom_call_target="tpu_custom_call", output_to_operand_aliasing={{}: (5, {})} | custom-call | flops 30064771072 | bytes 38797312 | tf_op jit(solution)/shard_map/wgrad_in/pallas_call | solution.py:342
  (364 shorter events, 420.4 us)
Async XLA Ops:
  7.2 38.6 %all-gather.12.cloned.1.call-start = ((), (), s32[]{:S(2)}) async-start(), calls=%async_computation.9 | async-start | bytes 4718592 | tf_op jit(solution)/shard_map/all_gather | solution.py:473
  9.2 79.6 %all-gather.14.cloned.1.call-start = ((), (), s32[]{:S(2)}) async-start(), calls=%async_computation.10 | async-start | bytes 9437184 | tf_op jit(solution)/shard_map/all_gather | solution.py:463
  26.7 109.9 %all-gather.10.cloned.1.call-start = ((), (), s32[]{:S(2)}) async-start(), calls=%async_computation.8 | async-start | bytes 9437184 | tf_op jit(solution)/shard_map/all_gather | solution.py:463
  27.5 245.3 %reduce-scatter.11.cloned.1.call-start = ((), (), s32[]{:S(2)}) async-start(), calls=%async_computation.12 | async-start | bytes 9437184 | tf_op jit(solution)/shard_map/reduce_scatter | solution.py:466
  192.6 98.8 %reduce-scatter.9.cloned.1.call-start = ((), (), s32[]{:S(2)}) async-start(), calls=%async_computation.11 | async-start | bytes 9437184 | tf_op jit(solution)/shard_map/reduce_scatter | solution.py:466
  225.3 119.2 %all-gather.18.cloned.1.call-start = ((), (), s32[]{:S(2)}) async-start(), calls=%async_computation.14 | async-start | bytes 9437184 | tf_op jit(solution)/shard_map/all_gather | solution.py:463
  256.1 37.9 %copy-start.32 = (f32[1,2048]{1,0:T(1,128)}, f32[1,2048]{1,0:T(1,128)S(1)}, u32[]{:S(2)}) copy-start(f32[1,2048]{1,0:T(1,128)S(1)} %get-tuple-element.288) | copy-start | bytes 24580
  298.4 93.9 %all-gather.16.cloned.1.call-start = ((), (), s32[]{:S(2)}) async-start(), calls=%async_computation.13 | async-start | bytes 9437184 | tf_op jit(solution)/shard_map/all_gather | solution.py:463
  299.2 181.3 %all-gather.20.cloned.1.call-start = ((), (), s32[]{:S(2)}) async-start(), calls=%async_computation.15 | async-start | bytes 9437184 | tf_op jit(solution)/shard_map/all_gather | solution.py:463
  301.0 47.5 %copy-start.73 = (f32[1,256]{1,0:T(1,128)S(1)}, f32[1,256]{1,0:T(1,128)}, u32[]{:S(2)}) copy-start(f32[1,256]{1,0:T(1,128)} %get-tuple-element.305) | copy-start | bytes 3076
  301.0 47.9 %copy-start.74 = (f32[1,256]{1,0:T(1,128)S(1)}, f32[1,256]{1,0:T(1,128)}, u32[]{:S(2)}) copy-start(f32[1,256]{1,0:T(1,128)} %get-tuple-element.303) | copy-start | bytes 3076
  347.6 155.0 %all-gather.22.cloned.1.call-start = ((), (), s32[]{:S(2)}) async-start(), calls=%async_computation.16 | async-start | bytes 9437184 | tf_op jit(solution)/shard_map/all_gather | solution.py:463
  348.4 330.3 %reduce-scatter.17.cloned.1.call-start = ((), (), s32[]{:S(2)}) async-start(), calls=%async_computation.19 | async-start | bytes 9437184 | tf_op jit(solution)/shard_map/reduce_scatter | solution.py:466
  480.6 198.2 %reduce-scatter.19.cloned.1.call-start = ((), (), s32[]{:S(2)}) async-start(), calls=%async_computation.20 | async-start | bytes 9437184 | tf_op jit(solution)/shard_map/reduce_scatter | solution.py:466
  481.3 200.6 %reduce-scatter.13.cloned.1.call-start = ((), (), s32[]{:S(2)}) async-start(), calls=%async_computation.17 | async-start | bytes 9437184 | tf_op jit(solution)/shard_map/reduce_scatter | solution.py:466
  609.1 98.9 %reduce-scatter.15.cloned.1.call-start = ((), (), s32[]{:S(2)}) async-start(), calls=%async_computation.18 | async-start | bytes 9437184 | tf_op jit(solution)/shard_map/reduce_scatter | solution.py:466
  639.1 147.8 %all-gather.24.cloned.1.call-start = ((), (), s32[]{:S(2)}) async-start(), calls=%async_computation.21 | async-start | bytes 9437184 | tf_op jit(solution)/shard_map/all_gather | solution.py:463
  721.7 96.4 %all-gather.26.cloned.1.call-start = ((), (), s32[]{:S(2)}) async-start(), calls=%async_computation.22 | async-start | bytes 9437184 | tf_op jit(solution)/shard_map/all_gather | solution.py:463
  722.4 305.5 %reduce-scatter.21.cloned.1.call-start = ((), (), s32[]{:S(2)}) async-start(), calls=%async_computation.23 | async-start | bytes 9437184 | tf_op jit(solution)/shard_map/reduce_scatter | solution.py:466
  924.4 103.5 %reduce-scatter.23.cloned.1.call-start = ((), (), s32[]{:S(2)}) async-start(), calls=%async_computation.24 | async-start | bytes 9437184 | tf_op jit(solution)/shard_map/reduce_scatter | solution.py:466
  988.0 40.0 %copy-start.2 = (bf16[1,512,2048]{2,1,0:T(8,128)(2,1)S(1)}, bf16[1,512,2048]{2,1,0:T(8,128)(2,1)}, u32[]{:S(2)}) copy-start(bf16[1,512,2048]{2,1,0:T(8,128)(2,1)} %param.13) | copy-start | bytes 6291460
  988.0 40.0 %copy-start.31 = (f32[1,2048]{1,0:T(1,128)S(1)}, f32[1,2048]{1,0:T(1,128)}, u32[]{:S(2)}) copy-start(f32[1,2048]{1,0:T(1,128)} %copy-done.30) | copy-start | bytes 24580
  988.0 40.0 %copy-start.39 = (f32[512]{0:T(512)S(1)}, f32[512]{0:T(512)}, u32[]{:S(2)}) copy-start(f32[512]{0:T(512)} %copy-done.38) | copy-start | bytes 6148
  988.0 42.6 %copy-start.54 = (f32[512]{0:T(512)S(1)}, f32[512]{0:T(512)}, u32[]{:S(2)}) copy-start(f32[512]{0:T(512)} %copy-done.53) | copy-start | bytes 6148
  (70 other events, 750.0 us)
Sparse Core Ops, SparseCore 0:
  10.2 31.0 all-gather.11
  43.4 45.3 all-gather.13
  91.0 45.6 all-gather.9
  192.7 47.7 reduce-scatter.10
  243.3 48.0 reduce-scatter.8
  298.5 45.9 all-gather.17
  346.6 45.6 all-gather.15
  393.9 45.6 all-gather.19
  441.2 45.6 all-gather.21
  489.0 47.7 reduce-scatter.16
  539.7 48.0 reduce-scatter.18
  609.2 47.7 reduce-scatter.12
  659.9 48.0 reduce-scatter.14
  721.8 49.0 all-gather.23
  772.4 45.6 all-gather.25
  924.5 47.7 reduce-scatter.20
  974.5 48.0 reduce-scatter.22
